TPU v7x, 256 devices: a whole 4x4x8 slice. The times are simulated.
256 devices in a mesh: dp: 4 (over y_lo, core), sp: 8 (over y_hi, x), tp: 8 (over z).
Axes of the slice: x: 4, y: 4 (y_hi: 2, y_lo: 2; y = y_hi * 2 + y_lo), z: 8, core: 2. Of those that a mesh axis runs over, the one named last changes fastest.
Arguments:
- query: bfloat16 [4, 3072, 3072], P('dp', 'sp', 'tp'), may hold values from -110 to 110
- key: bfloat16 [4, 3072, 3072], P('dp', 'sp', 'tp'), may hold values from -8 to 8
- value: bfloat16 [4, 3072, 3072], P('dp', 'sp', 'tp'), may hold values from -6 to 6
- text_key: bfloat16 [4, 256, 3072], P('dp', None, 'tp'), may hold values from -6 to 6
- text_value: bfloat16 [4, 256, 3072], P('dp', None, 'tp'), may hold values from -6 to 6
- grad_out: bfloat16 [4, 3072, 3072], P('dp', 'sp', 'tp'), may hold values from -6 to 6
- gate: bfloat16 [4, 3072], P('dp'), may hold values from 0.5 to 1.5
- out_weight: bfloat16 [3072, 3072], P('tp', 'dp'), may hold values from -0.109375 to 0.109375
- windows: int32 [8, 2], P('sp'), may hold values from 0 to 2, as said below
- tile_map: int32 [8, 1], replicated, may hold values from 0 to 2, as said below
- text_count: int32 [4], P('dp'), may hold values from 1 to 256
Outputs:
- grad_query: bfloat16 [4, 3072, 3072], P('dp', 'sp', 'tp')
- grad_key: bfloat16 [4, 3072, 3072], P('dp', 'sp', 'tp')
- grad_value: bfloat16 [4, 3072, 3072], P('dp', 'sp', 'tp')
- grad_text_key: bfloat16 [4, 256, 3072], P('dp', None, 'tp')
- grad_text_value: bfloat16 [4, 256, 3072], P('dp', None, 'tp')
- grad_weight: float32 [3072, 3072], P('tp', 'dp')
Inputs may be any that keep to these rules, and one draw needn't show every extreme that they name: `tile_map`: the positions within each row are distinct. `windows`: the time reach is 0 or 1; the first tile of every time slab has time reach 1 and spatial reach 2.
All inputs are finite; a program needn't handle non-finite values.
Results may differ from a plain program's by a relative error of at most 0.024.
Values may be sent and summed in bfloat16 or wider, within the bound.
A program may use at most 64 MiB of HBM per device.

v0:
```python
import functools

import jax
import jax.numpy as jnp
from jax import lax
from jax.experimental import pallas as pl
from jax.experimental.pallas import tpu as pltpu
from jax.sharding import PartitionSpec as P

HD = 128
VMEM = 67043328
MESH = pl.DeviceIdType.MESH

NT = (((1,), (1,)), ((), ()))
NN = (((1,), (0,)), ((), ()))
TN = (((0,), (0,)), ((), ()))

bf16, f32 = jnp.bfloat16, jnp.float32


def mm(a, b, dims):
    return lax.dot_general(a, b, dims, preferred_element_type=f32)


def item_k(h):
    return 3 * h


def item_v(h):
    return 3 * h + 1


def item_q(h):
    return 3 * h + 2


def kernel(
    names,
    *refs,
):
    r_ = dict(zip(names, refs, strict=True))
    q_ref, k_ref, v_ref, tk_ref, tv_ref = (r_[n] for n in ("q", "k", "v", "tk", "tv"))
    s_ref, w_ref, gate_ref, win_ref = (r_[n] for n in ("s", "w", "gate", "win"))
    map_ref, live_ref = r_["map"], r_["live"]
    keys, vals, qf, gaf = r_["keys"], r_["vals"], r_["qf"], r_["gaf"]
    st_out, st_in, dl_out, dl_in = r_["st_out"], r_["st_in"], r_["dl_out"], r_["dl_in"]
    raw, nat, w_all, acc = r_["raw"], r_["nat"], r_["w_all"], r_["acc"]
    ga_t, att_t, wts, wfar, gs_buf = r_["ga_t"], r_["att_t"], r_["wts"], r_["wfar"], r_["gs_buf"]
    parts, g1_out, g1_in = r_["parts"], r_["g1_out"], r_["g1_in"]
    gy_out, gy_in, gx_out, gx_in = r_["gy_out"], r_["gy_in"], r_["gx_out"], r_["gx_in"]
    ag_out, gfin = r_["ag_out"], r_["gfin"]
    tx_out, tx_in, tg = r_["tx_out"], r_["tx_in"], r_["tg"]
    gk_sum, gv_sum = r_["gk_sum"], r_["gv_sum"]

    factor = HD ** (-0.5)
    tok, width = q_ref.shape
    text = tk_ref.shape[0]
    heads = width // HD
    near = tok + text
    n_tp = n_sp = 8
    me_sp = lax.axis_index("sp")
    me_dp = lax.axis_index("dp")
    me_tp = lax.axis_index("tp")
    x = me_sp & 3
    yh = me_sp >> 2
    core = me_dp & 1
    yl = me_dp >> 1
    w = s_ref.shape[1]
    piece = width // n_sp
    half = width // 2
    has = [me_sp >= 1, me_sp + 1 < n_sp]
    side_sp = [me_sp - 1, me_sp + 1]

    partners = [{"tp": (me_tp + 1) & 7}, {"tp": (me_tp + 7) & 7}]
    partners += [{"dp": me_dp ^ 1}, {"dp": me_dp ^ 2}, {"dp": me_dp ^ 2, "sp": me_sp ^ 4}]
    partners += [{"sp": me_sp ^ j} for j in range(1, n_sp)]
    barrier = pltpu.get_barrier_semaphore()
    for where in partners:
        pl.semaphore_signal(barrier, inc=1, device_id=where, device_id_type=MESH)
    pl.semaphore_wait(barrier, len(partners))

    def remote(src, dst, send, recv, where):
        return pltpu.make_async_remote_copy(
            src_ref=src,
            dst_ref=dst,
            send_sem=send,
            recv_sem=recv,
            device_id=where,
            device_id_type=MESH,
        )

    chunk = tok // 2

    def crow(c):
        return pl.ds(c * chunk, chunk)

    def z_copy(up, t, c):
        r = (8 - t) % 8 if up else t
        to = (r + 7) % 8 if up else (r + 1) % 8
        src = s_ref.at[crow(c)] if t == 0 else raw.at[r, crow(c)]
        send = r_["zs"].at[0 if up else 1, t, c]
        recv = r_["zr"].at[0 if up else 1, t, c]
        where = {"tp": (me_tp + (1 if up else 7)) & 7}
        return remote(src, raw.at[to, crow(c)], send, recv, where)

    def z_exists(up, t, c):
        return t < 3 or (t == 3 and c == (0 if up else 1))

    def z_arrive(t, c):
        for up in (True, False):
            if z_exists(up, t, c):
                z_copy(up, t, c).wait_recv()
                if t < 3 and z_exists(up, t + 1, c):
                    z_copy(up, t + 1, c).start()

    def w_core():
        return remote(w_ref, w_all.at[me_dp], r_["ws"].at[0], r_["wr"].at[0], {"dp": me_dp ^ 1})

    def w_y(i):
        rows = pl.ds(i * half, half)
        where = {"dp": me_dp ^ 2, "sp": me_sp ^ (4 * i)}
        return remote(
            w_ref.at[rows], w_all.at[me_dp, rows], r_["ws"].at[1 + i], r_["wr"].at[1 + i], where
        )

    def w_fwd():
        block = w_all.at[me_dp ^ 2]
        return remote(block, block, r_["ws"].at[3], r_["wr"].at[3], {"dp": me_dp ^ 1})

    def halo(side, item):
        there = 1 - side
        region = pl.ds(near + there * tok, tok)
        if item < 3 * heads:
            h, kind = divmod(item, 3)
            c = pl.ds(h * HD, HD)
            src = (k_ref, v_ref, q_ref)[kind].at[:, c]
            dst = (keys.at[region, c], vals.at[region, c], qf.at[there, :, c])[kind]
        elif item < 4 * heads:
            c = pl.ds((item - 3 * heads) * HD, HD)
            src, dst = ga_t.at[c], gaf.at[there, c]
        elif item == 4 * heads:
            src, dst = st_out.at[side], st_in.at[there]
        else:
            src, dst = dl_out, dl_in.at[there]
        return remote(
            src, dst, r_["hs"].at[side, item], r_["hr"].at[there, item], {"sp": side_sp[side]}
        )

    def halo_start(items):
        for side in (0, 1):

            @pl.when(has[side])
            def _():
                for item in items:
                    halo(side, item).start()

    def halo_wait(side, items):
        for item in items:
            c = halo(1 - side, item)
            c.wait_recv()

    def halo_wait_both(items):
        for side in (0, 1):

            @pl.when(has[side])
            def _():
                halo_wait(side, items)

    for c in (0, 1):
        z_copy(True, 0, c).start()
        z_copy(False, 0, c).start()
    w_core().start()
    w_y(0).start()
    w_y(1).start()
    for h in range(heads):
        halo_start([item_k(h), item_v(h)])
    for h in range(heads):
        halo_start([item_q(h)])

    keys[:tok] = k_ref[...]
    keys[tok:near] = tk_ref[...]
    vals[:tok] = v_ref[...]
    vals[tok:near] = tv_ref[...]
    w_all[me_dp] = w_ref[...]
    for side in (0, 1):

        @pl.when(jnp.logical_not(has[side]))
        def _():
            region = slice(near + side * tok, near + (side + 1) * tok)
            keys[region] = jnp.zeros((tok, width), bf16)
            vals[region] = jnp.zeros((tok, width), bf16)

    def blk(r):
        return (me_tp + r) & 7

    def scale(r):
        gate = gate_ref[:, pl.ds(pl.multiple_of(blk(r) * w, HD), w)].astype(f32)
        src = s_ref[...] if r == 0 else raw[r]
        nat[r] = (src.astype(f32) * gate).astype(bf16)

    def ga_add(r, first=False):
        at = pl.multiple_of((blk(r) & 1) * w, HD)
        term = mm(w_all[blk(r) >> 1, :, pl.ds(at, w)], nat[r], NT)
        if first:
            acc[...] = term
        else:
            acc[...] += term

    place = map_ref[me_sp, 0]
    side_bias = []
    for side in (0, 1):
        other = map_ref[jnp.clip(side_sp[side], 0, n_sp - 1), 0]
        seen = (win_ref[0:1, 0:1] >= 1) & (win_ref[0:1, 1:2] >= jnp.abs(place - other))
        edge = jnp.where(has[side], 0.0, -1e30).astype(f32)
        side_bias.append(jnp.minimum(jnp.where(seen, 0.0, -1e30).astype(f32), edge))
    place_of = lax.broadcasted_iota(jnp.int32, (text, 1), 0)
    words = jnp.where(place_of < live_ref[0], 0.0, -1e30).astype(f32)
    bias_ref = r_["bias"]
    bias_ref[:tok] = jnp.zeros((tok, 1), f32)
    bias_ref[tok:near] = words
    for side in (0, 1):
        region = slice(near + side * tok, near + (side + 1) * tok)
        bias_ref[region] = jnp.broadcast_to(side_bias[side], (tok, 1))

    def cols(h):
        return slice(h * HD, (h + 1) * HD)

    def forward(h):
        c = cols(h)
        scores = factor * mm(keys[:, c], q_ref[:, c], NT) + bias_ref[...]
        top = jnp.max(scores, axis=0, keepdims=True)
        e = jnp.exp(scores - top)
        inv = 1.0 / jnp.sum(e, axis=0, keepdims=True)
        weights = e * inv
        wts[h] = weights
        att_t[c, :] = mm(vals[:, c], weights.astype(bf16), TN).astype(bf16)
        for side in (0, 1):
            st_out[side, h : h + 1, :] = top - side_bias[side]
            st_out[side, heads + h : heads + h + 1, :] = inv

    def far_weights(side, h):
        c = cols(h)
        scores = factor * mm(keys[:tok, c], qf[side, :, c], NT)
        e = jnp.exp(scores - st_in[side, h : h + 1, :])
        wfar[side, h] = e * st_in[side, heads + h : heads + h + 1, :]

    def core_owns(r):
        return ((blk(r) >> 1) & 1) == core

    def mine(r):
        return (blk(r) >> 1) == me_dp

    def core_only(r):
        return core_owns(r) & ((blk(r) >> 2) != yl)

    def s1_copy(r):
        return remote(
            g1_out.at[r], g1_in.at[r], r_["s1s"].at[r], r_["s1r"].at[r], {"dp": me_dp ^ 1}
        )

    def gy_over(r, i):
        rows = pl.ds(i * half, half)
        return remote(
            gy_out.at[r, rows],
            gy_in.at[r, yh],
            r_["gys"].at[r, i],
            r_["gyr"].at[r, yh],
            {"dp": me_dp ^ 2, "sp": x + 4 * i},
        )

    def gy_across(r):
        rows = pl.ds(pl.multiple_of((1 - yh) * half, half), half)
        return remote(
            gy_out.at[r, rows],
            gy_in.at[r, 2],
            r_["gys"].at[r, 2],
            r_["gyr"].at[r, 2],
            {"sp": me_sp ^ 4},
        )

    def gx_copy(r, j):
        rows = pl.ds(pl.multiple_of((x ^ j) * piece, piece), piece)
        return remote(
            gx_out.at[r, rows],
            gx_in.at[r, j - 1],
            r_["gxs"].at[r, j - 1],
            r_["gxr"].at[r, j - 1],
            {"sp": me_sp ^ j},
        )

    def ag_copy(r, j):
        rows = pl.ds(pl.multiple_of(me_sp * piece, piece), piece)
        return remote(
            ag_out.at[r],
            gfin.at[blk(r) & 1, rows],
            r_["ags"].at[r, j - 1],
            r_["agr"].at[r, j - 1],
            {"sp": me_sp ^ j},
        )

    def gw_part(r):
        parts[r] = mm(att_t[...], nat[r], NN)

        @pl.when(jnp.logical_not(core_owns(r)))
        def _():
            g1_out[r] = parts[r].astype(bf16)
            s1_copy(r).start()

    def gw_s1(r):
        @pl.when(core_owns(r))
        def _():
            s1_copy(r).wait_recv()
            total = parts[r] + g1_in[r].astype(f32)
            parts[r] = total
            gy_out[r] = total.astype(bf16)

        @pl.when(core_only(r))
        def _():
            gy_over(r, 0).start()
            gy_over(r, 1).start()

        @pl.when(mine(r))
        def _():
            gy_across(r).start()

    def gw_sy(r):
        @pl.when(mine(r))
        def _():
            for i in range(3):
                remote(
                    gy_out.at[r, pl.ds(0, half)],
                    gy_in.at[r, i],
                    r_["gys"].at[r, i],
                    r_["gyr"].at[r, i],
                    {"sp": me_sp ^ 4},
                ).wait_recv()
            total = parts[r, pl.ds(pl.multiple_of(yh * half, half), half), :]
            for i in range(3):
                total = total + gy_in[r, i].astype(f32)
            parts[r, :half, :] = total
            gx_out[r] = total.astype(bf16)
            for j in range(1, 4):
                gx_copy(r, j).start()

    def gw_sx(r):
        @pl.when(mine(r))
        def _():
            for j in range(1, 4):
                gx_copy(r, j).wait_recv()
            total = parts[r, pl.ds(pl.multiple_of(x * piece, piece), piece), :]
            for j in range(3):
                total = total + gx_in[r, j].astype(f32)
            ag_out[r] = total.astype(bf16)
            gfin[blk(r) & 1, pl.ds(pl.multiple_of(me_sp * piece, piece), piece), :] = total.astype(
                bf16
            )
            for j in range(1, n_sp):
                ag_copy(r, j).start()

    gw_v = r_["gw_v"]

    def gw_ag(r):
        @pl.when(mine(r))
        def _():
            for j in range(1, n_sp):
                ag_copy(r, j).wait_recv()
            at = pl.ds(pl.multiple_of((blk(r) & 1) * w, HD), w)
            gw_v[:, at] = gfin[blk(r) & 1].astype(f32)

    trow = text // n_sp

    def tx_copy(j):
        return remote(
            tx_out.at[me_sp ^ j],
            tx_in.at[j - 1],
            r_["txs"].at[j - 1],
            r_["txr"].at[j - 1],
            {"sp": me_sp ^ j},
        )

    def tg_copy(j):
        return remote(
            tg.at[me_sp],
            tg.at[me_sp],
            r_["tgs"].at[j - 1],
            r_["tgr"].at[j - 1],
            {"sp": me_sp ^ j},
        )

    gq_v, gk_v, gv_v, gtk_v, gtv_v = (r_[n] for n in ("gq_v", "gk_v", "gv_v", "gtk_v", "gtv_v"))

    def text_part(h):
        c = cols(h)
        ga = ga_t[c, :]
        wt = wts[h, tok:near, :]
        gp = mm(vals[tok:near, c], ga, NN)
        gs = (wt * (gp - dl_out[h : h + 1, :])).astype(bf16)
        gs_buf[h, tok:near, :] = gs
        gk = (factor * mm(gs, q_ref[:, c], NN)).astype(bf16)
        gv = mm(wt.astype(bf16), ga, NT).astype(bf16)
        for j in range(n_sp):
            rows = slice(j * trow, (j + 1) * trow)
            tx_out[j, :trow, c] = gk[rows]
            tx_out[j, trow:, c] = gv[rows]

    def own_part(h):
        c = cols(h)
        ga = ga_t[c, :]
        delta = dl_out[h : h + 1, :]
        for lo, hi in ((0, tok), (near, near + 2 * tok)):
            gp = mm(vals[lo:hi, c], ga, NN)
            gs_buf[h, lo:hi, :] = (wts[h, lo:hi, :] * (gp - delta)).astype(bf16)
        gq_v[:, c] = (factor * mm(keys[:, c], gs_buf[h], TN)).T.astype(bf16)
        gk_sum[:, c] = mm(gs_buf[h, :tok, :], q_ref[:, c], NN)
        gv_sum[:, c] = mm(wts[h, :tok, :].astype(bf16), ga, NT)

    def far_part(side, h):
        c = cols(h)
        ga = gaf[side, c, :]
        weights = wfar[side, h]
        gp = mm(vals[:tok, c], ga, NN)
        gs = (weights * (gp - dl_in[side, h : h + 1, :])).astype(bf16)
        gk_sum[:, c] += mm(gs, qf[side, :, c], NN)
        gv_sum[:, c] += mm(weights.astype(bf16), ga, NT)

    scale(0)
    z_arrive(0, 0)
    w_core().wait_recv()
    z_arrive(0, 1)
    w_y(0).wait_recv()
    w_y(1).wait_recv()
    w_fwd().start()
    scale(1)
    scale(7)
    halo_wait_both([item_k(0), item_v(0)])
    forward(0)
    w_fwd().wait_recv()
    ga_add(0, True)
    z_arrive(1, 0)
    halo_wait_both([item_k(1), item_v(1)])
    forward(1)
    ga_add(1)
    ga_add(7)
    z_arrive(1, 1)
    scale(2)
    scale(6)
    halo_wait_both([item_k(2), item_v(2)])
    forward(2)
    halo_start([4 * heads])
    z_arrive(2, 0)
    for r in (0, 1, 7):
        gw_part(r)
    ga_add(2)
    ga_add(6)
    for r in (0, 1, 7):
        gw_s1(r)
    for r in (2, 6):
        gw_part(r)
    z_arrive(2, 1)
    scale(3)
    scale(5)
    for r in (3, 5):
        gw_part(r)
    for r in (2, 6):
        gw_s1(r)
    ga_add(3)
    ga_add(5)
    for r in (0, 1, 7):
        gw_sy(r)
    halo_wait_both([4 * heads])
    for h in range(heads):
        halo_wait_both([item_q(h)])
        for side in (0, 1):
            pl.when(has[side])(functools.partial(far_weights, side, h))
    for r in (3, 5):
        gw_s1(r)
    for r in (2, 6):
        gw_sy(r)
    for r in (0, 1, 7):
        gw_sx(r)
    z_arrive(3, 0)
    z_arrive(3, 1)
    scale(4)
    ga_add(4)
    ga_t[...] = acc[...].astype(bf16)
    for h in range(heads):
        c = cols(h)
        dl_out[h : h + 1, :] = jnp.sum(
            ga_t[c, :].astype(f32) * att_t[c, :].astype(f32), axis=0, keepdims=True
        )
    gw_part(4)
    for h in range(heads):
        text_part(h)
    for j in range(1, n_sp):
        tx_copy(j).start()
    halo_start([4 * heads + 1] + [3 * heads + h for h in range(heads)])
    gw_s1(4)
    own_part(0)
    for r in (3, 5):
        gw_sy(r)
    for r in (2, 6):
        gw_sx(r)
    own_part(1)
    gw_sy(4)
    for r in (3, 5):
        gw_sx(r)
    own_part(2)
    gq_store = pltpu.make_async_copy(gq_v, r_["gq_out"], r_["os"].at[0])
    gq_store.start()
    for j in range(1, n_sp):
        tx_copy(j).wait_recv()
    total = tx_out[me_sp].astype(f32)
    for j in range(n_sp - 1):
        total = total + tx_in[j].astype(f32)
    tg[me_sp] = total.astype(bf16)
    for j in range(1, n_sp):
        tg_copy(j).start()
    gw_sx(4)
    for r in (0, 1, 7, 2, 6, 3, 5):
        gw_ag(r)
    halo_wait_both([4 * heads + 1])
    for h in range(heads):
        halo_wait_both([3 * heads + h])
        for side in (0, 1):
            pl.when(has[side])(functools.partial(far_part, side, h))
        c = cols(h)
        gk_v[:, c] = (factor * gk_sum[:, c]).astype(bf16)
        gv_v[:, c] = gv_sum[:, c].astype(bf16)
    stored = [
        pltpu.make_async_copy(gk_v, r_["gk_out"], r_["os"].at[1]),
        pltpu.make_async_copy(gv_v, r_["gv_out"], r_["os"].at[2]),
    ]
    for c in stored:
        c.start()
    for j in range(1, n_sp):
        remote(
            tg.at[me_sp],
            tg.at[me_sp ^ j],
            r_["tgs"].at[j - 1],
            r_["tgr"].at[j - 1],
            {"sp": me_sp ^ j},
        ).wait_recv()
    for j in range(n_sp):
        rows = slice(j * trow, (j + 1) * trow)
        gtk_v[rows] = tg[j, :trow]
        gtv_v[rows] = tg[j, trow:]
    late = [
        pltpu.make_async_copy(gtk_v, r_["gtk_out"], r_["os"].at[3]),
        pltpu.make_async_copy(gtv_v, r_["gtv_out"], r_["os"].at[4]),
    ]
    for c in late:
        c.start()
    gw_ag(4)
    gw_store = pltpu.make_async_copy(gw_v, r_["gw_out"], r_["os"].at[5])
    gw_store.start()

    for up in (True, False):
        for t in range(4):
            for c in (0, 1):
                if z_exists(up, t, c):
                    z_copy(up, t, c).wait_send()
    w_core().wait_send()
    w_y(0).wait_send()
    w_y(1).wait_send()
    w_fwd().wait_send()
    for side in (0, 1):

        @pl.when(has[side])
        def _():
            for item in range(4 * heads + 2):
                halo(side, item).wait_send()

    for r in range(n_tp):

        @pl.when(jnp.logical_not(core_owns(r)))
        def _():
            s1_copy(r).wait_send()

        @pl.when(core_only(r))
        def _():
            gy_over(r, 0).wait_send()
            gy_over(r, 1).wait_send()

        @pl.when(mine(r))
        def _():
            gy_across(r).wait_send()
            for j in range(1, 4):
                gx_copy(r, j).wait_send()
            for j in range(1, n_sp):
                ag_copy(r, j).wait_send()

    for j in range(1, n_sp):
        tx_copy(j).wait_send()
        tg_copy(j).wait_send()
    for c in [gq_store] + stored + late + [gw_store]:
        c.wait()


def call(q, k, v, tk, tv, s, w, gate, windows, tile_map, text_count):
    tok, width = q.shape
    text = tk.shape[0]
    heads = width // HD
    cols = w.shape[1]
    total = 3 * tok + text
    block = s.shape[1]
    piece, half = width // 8, width // 2
    sm = pl.BlockSpec(memory_space=pltpu.SMEM)
    vm = pl.BlockSpec(memory_space=pltpu.VMEM)
    outs = [
        ("gq", (tok, width), bf16),
        ("gk", (tok, width), bf16),
        ("gv", (tok, width), bf16),
        ("gtk", (text, width), bf16),
        ("gtv", (text, width), bf16),
        ("gw", (width, cols), f32),
    ]
    scratch = [(n + "_v", a, b) for n, a, b in outs] + [
        ("keys", (total, width), bf16),
        ("vals", (total, width), bf16),
        ("qf", (2, tok, width), bf16),
        ("gaf", (2, width, tok), bf16),
        ("st_out", (2, 8, tok), f32),
        ("st_in", (2, 8, tok), f32),
        ("dl_out", (8, tok), f32),
        ("dl_in", (2, 8, tok), f32),
        ("bias", (total, 1), f32),
        ("raw", (8, tok, block), bf16),
        ("nat", (8, tok, block), bf16),
        ("w_all", (4, width, cols), bf16),
        ("acc", (width, tok), f32),
        ("ga_t", (width, tok), bf16),
        ("att_t", (width, tok), bf16),
        ("wts", (heads, total, tok), f32),
        ("wfar", (2, heads, tok, tok), f32),
        ("gs_buf", (heads, total, tok), bf16),
        ("gk_sum", (tok, width), f32),
        ("gv_sum", (tok, width), f32),
        ("parts", (8, width, block), f32),
        ("g1_out", (8, width, block), bf16),
        ("g1_in", (8, width, block), bf16),
        ("gy_out", (8, width, block), bf16),
        ("gy_in", (8, 3, half, block), bf16),
        ("gx_out", (8, half, block), bf16),
        ("gx_in", (8, 3, piece, block), bf16),
        ("ag_out", (8, piece, block), bf16),
        ("gfin", (2, width, block), bf16),
        ("tx_out", (8, text // 4, width), bf16),
        ("tx_in", (7, text // 4, width), bf16),
        ("tg", (8, text // 4, width), bf16),
    ]
    items = 4 * heads + 2
    sems = [
        ("zs", (2, 4, 2)),
        ("zr", (2, 4, 2)),
        ("ws", (4,)),
        ("wr", (4,)),
        ("hs", (2, items)),
        ("hr", (2, items)),
        ("s1s", (8,)),
        ("s1r", (8,)),
        ("gys", (8, 3)),
        ("gyr", (8, 3)),
        ("gxs", (8, 3)),
        ("gxr", (8, 3)),
        ("ags", (8, 7)),
        ("agr", (8, 7)),
        ("txs", (7,)),
        ("txr", (7,)),
        ("tgs", (7,)),
        ("tgr", (7,)),
        ("os", (6,)),
    ]
    args = ["q", "k", "v", "tk", "tv", "s", "w", "gate", "win", "map", "live"]
    names = args + [n + "_out" for n, _, _ in outs] + [n for n, _, _ in scratch]
    names += [n for n, _ in sems]
    return pl.pallas_call(
        functools.partial(kernel, tuple(names)),
        out_shape=[jax.ShapeDtypeStruct(a, b) for _, a, b in outs],
        in_specs=[vm] * 9 + [sm] * 2,
        out_specs=[pl.BlockSpec(memory_space=pl.ANY)] * len(outs),
        scratch_shapes=[pltpu.VMEM(a, b) for _, a, b in scratch]
        + [pltpu.SemaphoreType.DMA(n) for _, n in sems],
        compiler_params=pltpu.CompilerParams(
            collective_id=0, has_side_effects=True, vmem_limit_bytes=VMEM
        ),
        name="attention_backward",
    )(q, k, v, tk, tv, s, w, gate, windows, tile_map, text_count)


def copy_kernel(n, *refs):
    srcs, dsts, held = refs[:n], refs[n : 2 * n], refs[2 * n : 3 * n]
    in_sem, out_sem = refs[3 * n :]
    loads = [pltpu.make_async_copy(srcs[i], held[i], in_sem.at[i]) for i in range(n)]
    stores = [pltpu.make_async_copy(held[i], dsts[i], out_sem.at[i]) for i in range(n)]
    for c in loads:
        c.start()
    for i in range(n):
        loads[i].wait()
        stores[i].start()
    for c in stores:
        c.wait()


def copy_call(arrays):
    n = len(arrays)
    hbm = pl.BlockSpec(memory_space=pltpu.HBM)
    return pl.pallas_call(
        functools.partial(copy_kernel, n),
        out_shape=[jax.ShapeDtypeStruct(a.shape, a.dtype) for a in arrays],
        in_specs=[hbm] * n,
        out_specs=[hbm] * n,
        scratch_shapes=[pltpu.VMEM(a.shape, a.dtype) for a in arrays]
        + [pltpu.SemaphoreType.DMA((n,))] * 2,
        compiler_params=pltpu.CompilerParams(vmem_limit_bytes=VMEM),
        name="results",
    )(*arrays)


def per_device(
    query,
    key,
    value,
    text_key,
    text_value,
    grad_out,
    gate,
    out_weight,
    windows,
    tile_map,
    text_count,
):
    outs = call(
        query[0],
        key[0],
        value[0],
        text_key[0],
        text_value[0],
        grad_out[0],
        out_weight,
        gate,
        windows,
        tile_map,
        text_count,
    )
    outs = copy_call(outs)
    return tuple(o[None] for o in outs[:5]) + (outs[5],)


def solution(mesh):
    placed = (
        P("dp", "sp", "tp"),
        P("dp", "sp", "tp"),
        P("dp", "sp", "tp"),
        P("dp", None, "tp"),
        P("dp", None, "tp"),
        P("dp", "sp", "tp"),
        P("dp", None),
        P("tp", "dp"),
        P("sp", None),
        P(),
        P("dp"),
    )
    return jax.shard_map(
        per_device,
        mesh=mesh,
        in_specs=placed,
        out_specs=(
            P("dp", "sp", "tp"),
            P("dp", "sp", "tp"),
            P("dp", "sp", "tp"),
            P("dp", None, "tp"),
            P("dp", None, "tp"),
            P("tp", "dp"),
        ),
        check_vma=False,
    )
```

profile of v0, /device:TPU:8, one launch (start us, length us, event | category | flops | bytes accessed | tf_op | source)
XLA Modules:
  0.0 106.7 jit_solution(4902349131896666909)
XLA Ops:
  1.3 1.3 %copy.17.refs_9_ = s32[8,1]{1,0:T(8,128)} copy(s32[8,1]{0,1:T(1,128)} %param.20) | data formatting | bytes 64 | tf_op args[9]
  2.6 101.2 %attention_backward.1 = (bf16[384,384]{1,0:T(8,128)(2,1)}, bf16[384,384]{1,0:T(8,128)(2,1)}, bf16[384,384]{1,0:T(8,128)(2,1)}, bf16[256,384]{1,0:T(8,128)(2,1)},...) custom-call(bf16[384,384]{1,0:T(8,128)(2,1)} %bitcast.11, bf16[384,384]{1,0:T(8,128)(2,1)} %bitcast.12, ...), custom_call_target="tpu_custom_call" | custom-call | tf_op jit(solution)/shard_map/attention_backward/pallas_call | solution.py:676
  103.8 2.8 %results.1 = (bf16[384,384]{1,0:T(8,128)(2,1)}, bf16[384,384]{1,0:T(8,128)(2,1)}, bf16[384,384]{1,0:T(8,128)(2,1)}, bf16[256,384]{1,0:T(8,128)(2,1)}, bf16[256,384]{1,0:T(8,128)(2,1)}, /*index=5*/f32[384,768]{1,0:T(8,128)}) custom-call(bf16[384,384]{1,0:T(8,128)(2,1)} %get-tuple-element.18.refs_0_, bf16[384,384]{1,0:T(8,128)(2,1)} %get-tuple-element.19.refs_1_, ...), custom_call_target="tpu_custom_call" | custom-call | tf_op jit(solution)/shard_map/results/pallas_call | solution.py:707
where the time goes:
time: 108 us; the launch traced here: 107 us
  Pallas kernels  104 us (96%)
  between operations  1.45 us (1%)
  local copies, waits for them, and re-layouts  1.32 us (1%)
    pallas_call x1, Pallas kernels, call(): pl.pallas_call(functools.partial(kernel, tuple(names)), out_shape=[jax.Sh...  101 us
    pallas_call x1, Pallas kernels, copy_call(): pl.pallas_call(functools.partial(copy_kernel, n), out_shape=[jax.ShapeDty...  2.79 us

commit v1 on v0

--- a/solution.py
+++ b/solution.py
@@ -48,7 +48,7 @@
     ga_t, att_t, wts, wfar, gs_buf = r_["ga_t"], r_["att_t"], r_["wts"], r_["wfar"], r_["gs_buf"]
     parts, g1_out, g1_in = r_["parts"], r_["g1_out"], r_["g1_in"]
     gy_out, gy_in, gx_out, gx_in = r_["gy_out"], r_["gy_in"], r_["gx_out"], r_["gx_in"]
-    ag_out, gfin = r_["ag_out"], r_["gfin"]
+    fin_out, gfin = r_["fin_out"], r_["gfin"]
     tx_out, tx_in, tg = r_["tx_out"], r_["tx_in"], r_["tg"]
     gk_sum, gv_sum = r_["gk_sum"], r_["gv_sum"]
 
@@ -66,7 +66,8 @@
     core = me_dp & 1
     yl = me_dp >> 1
     w = s_ref.shape[1]
-    piece = width // n_sp
+    piece = width // 16
+    y = 2 * yh + yl
     half = width // 2
     has = [me_sp >= 1, me_sp + 1 < n_sp]
     side_sp = [me_sp - 1, me_sp + 1]
@@ -98,7 +99,7 @@
         r = (8 - t) % 8 if up else t
         to = (r + 7) % 8 if up else (r + 1) % 8
         src = s_ref.at[crow(c)] if t == 0 else raw.at[r, crow(c)]
-        send = r_["zs"].at[0 if up else 1, t, c]
+        send = r_["zs"].at[0]
         recv = r_["zr"].at[0 if up else 1, t, c]
         where = {"tp": (me_tp + (1 if up else 7)) & 7}
         return remote(src, raw.at[to, crow(c)], send, recv, where)
@@ -116,16 +117,27 @@
     def w_core():
         return remote(w_ref, w_all.at[me_dp], r_["ws"].at[0], r_["wr"].at[0], {"dp": me_dp ^ 1})
 
-    def w_y(i):
-        rows = pl.ds(i * half, half)
+    ends = (x == 0) | (x == 3)
+    gives = jnp.where(x == 0, yh == 1, yh == 0)
+
+    def w_y(i, j):
+        rows = pl.ds(j * half, half)
         where = {"dp": me_dp ^ 2, "sp": me_sp ^ (4 * i)}
         return remote(
-            w_ref.at[rows], w_all.at[me_dp, rows], r_["ws"].at[1 + i], r_["wr"].at[1 + i], where
-        )
+            w_ref.at[rows],
+            w_all.at[me_dp, rows],
+            r_["ws"].at[1],
+            r_["wr"].at[1],
+            where,
+        )
+
+    def w_y_all(n):
+        held = w_all.at[pl.ds(0, n)]
+        return remote(held, held, r_["ws"].at[1], r_["wr"].at[1], {"dp": me_dp ^ 2})
 
     def w_fwd():
         block = w_all.at[me_dp ^ 2]
-        return remote(block, block, r_["ws"].at[3], r_["wr"].at[3], {"dp": me_dp ^ 1})
+        return remote(block, block, r_["ws"].at[2], r_["wr"].at[2], {"dp": me_dp ^ 1})
 
     def halo(side, item):
         there = 1 - side
@@ -142,8 +154,14 @@
             src, dst = st_out.at[side], st_in.at[there]
         else:
             src, dst = dl_out, dl_in.at[there]
+        if item < 4 * heads:
+            send = 0
+            got = (h if kind < 2 else heads) if item < 3 * heads else item - 2 * heads + 1
+        else:
+            send = 1 + item - 4 * heads
+            got = item - 2 * heads + 1
         return remote(
-            src, dst, r_["hs"].at[side, item], r_["hr"].at[there, item], {"sp": side_sp[side]}
+            src, dst, r_["hs"].at[side, send], r_["hr"].at[there, got], {"sp": side_sp[side]}
         )
 
     def halo_start(items):
@@ -154,24 +172,41 @@
                 for item in items:
                     halo(side, item).start()
 
-    def halo_wait(side, items):
-        for item in items:
-            c = halo(1 - side, item)
-            c.wait_recv()
-
-    def halo_wait_both(items):
+    def halo_wait(side, what):
+        kind, h = what
+        if kind in ("st", "dl"):
+            halo(1 - side, 4 * heads + (kind == "dl")).wait_recv()
+        elif kind == "ga":
+            halo(1 - side, 3 * heads + h).wait_recv()
+        else:
+            some = keys.at[pl.ds(0, 2 * tok), pl.ds(0, HD)] if kind == "kv" else qf.at[side]
+            got = r_["hr"].at[side, h if kind == "kv" else heads]
+            remote(some, some, r_["hs"].at[side, 0], got, {"sp": me_sp ^ 1}).wait_recv()
+
+    def halo_wait_both(*whats):
         for side in (0, 1):
 
             @pl.when(has[side])
             def _():
-                halo_wait(side, items)
+                for what in whats:
+                    halo_wait(side, what)
 
     for c in (0, 1):
         z_copy(True, 0, c).start()
         z_copy(False, 0, c).start()
     w_core().start()
-    w_y(0).start()
-    w_y(1).start()
+
+    @pl.when(jnp.logical_not(ends))
+    def _():
+        w_y(0, 0).start()
+        w_y(1, 1).start()
+
+    @pl.when(ends & gives)
+    def _():
+        for i in (0, 1):
+            for j in (0, 1):
+                w_y(i, j).start()
+
     for h in range(heads):
         halo_start([item_k(h), item_v(h)])
     for h in range(heads):
@@ -206,11 +241,18 @@
         else:
             acc[...] += term
 
-    place = map_ref[me_sp, 0]
+    slab_of = lax.broadcasted_iota(jnp.int32, (1, n_sp), 1)
+
+    def place_of_slab(slab):
+        here = jnp.where(slab_of == slab, map_ref[...].astype(f32), 0.0)
+        return jnp.sum(here, axis=1, keepdims=True)
+
+    place = place_of_slab(me_sp)
+    reach = win_ref[...].astype(f32)
     side_bias = []
     for side in (0, 1):
-        other = map_ref[jnp.clip(side_sp[side], 0, n_sp - 1), 0]
-        seen = (win_ref[0:1, 0:1] >= 1) & (win_ref[0:1, 1:2] >= jnp.abs(place - other))
+        apart = jnp.abs(place - place_of_slab(side_sp[side]))
+        seen = (reach[0:1, 0:1] >= 1.0) & (reach[0:1, 1:2] >= apart)
         edge = jnp.where(has[side], 0.0, -1e30).astype(f32)
         side_bias.append(jnp.minimum(jnp.where(seen, 0.0, -1e30).astype(f32), edge))
     place_of = lax.broadcasted_iota(jnp.int32, (text, 1), 0)
@@ -250,53 +292,50 @@
     def mine(r):
         return (blk(r) >> 1) == me_dp
 
-    def core_only(r):
-        return core_owns(r) & ((blk(r) >> 2) != yl)
-
     def s1_copy(r):
         return remote(
-            g1_out.at[r], g1_in.at[r], r_["s1s"].at[r], r_["s1r"].at[r], {"dp": me_dp ^ 1}
-        )
-
-    def gy_over(r, i):
-        rows = pl.ds(i * half, half)
+            g1_out.at[r], g1_in.at[r], r_["s1s"].at[0], r_["s1r"].at[r], {"dp": me_dp ^ 1}
+        )
+
+    def gy_copy(r, j):
+        where = {"dp": me_dp ^ (2 * (j & 1)), "sp": me_sp ^ (2 * (j & 2))}
         return remote(
-            gy_out.at[r, rows],
-            gy_in.at[r, yh],
-            r_["gys"].at[r, i],
-            r_["gyr"].at[r, yh],
-            {"dp": me_dp ^ 2, "sp": x + 4 * i},
-        )
-
-    def gy_across(r):
-        rows = pl.ds(pl.multiple_of((1 - yh) * half, half), half)
+            gy_out.at[r, y ^ j],
+            gy_in.at[r, j - 1],
+            r_["gys"].at[0],
+            r_["gyr"].at[r],
+            where,
+        )
+
+    def gx_copy(r, j):
         return remote(
-            gy_out.at[r, rows],
-            gy_in.at[r, 2],
-            r_["gys"].at[r, 2],
-            r_["gyr"].at[r, 2],
-            {"sp": me_sp ^ 4},
-        )
-
-    def gx_copy(r, j):
-        rows = pl.ds(pl.multiple_of((x ^ j) * piece, piece), piece)
+            gx_out.at[r, x ^ j],
+            gx_in.at[r, j - 1],
+            r_["gxs"].at[0],
+            r_["gxr"].at[r],
+            {"sp": me_sp ^ j},
+        )
+
+    def ag1_copy(r, i):
         return remote(
-            gx_out.at[r, rows],
-            gx_in.at[r, j - 1],
-            r_["gxs"].at[r, j - 1],
-            r_["gxr"].at[r, j - 1],
-            {"sp": me_sp ^ j},
-        )
-
-    def ag_copy(r, j):
-        rows = pl.ds(pl.multiple_of(me_sp * piece, piece), piece)
+            fin_out.at[r],
+            gfin.at[blk(r) & 1, y, x],
+            r_["ag1s"].at[0],
+            r_["ag1r"].at[r],
+            {"dp": blk(r) >> 1, "sp": 4 * i + x},
+        )
+
+    def ag1_sends(r, i):
+        return core_owns(r) & jnp.logical_not(mine(r) & (yh == i))
+
+    def ag2_copy(r, j):
+        slab = gfin.at[blk(r) & 1, :, x]
         return remote(
-            ag_out.at[r],
-            gfin.at[blk(r) & 1, rows],
-            r_["ags"].at[r, j - 1],
-            r_["agr"].at[r, j - 1],
-            {"sp": me_sp ^ j},
-        )
+            slab, slab, r_["ag2s"].at[0], r_["ag2r"].at[r], {"sp": me_sp ^ j}
+        )
+
+    def all_of(some, send, recv):
+        return remote(some, some, send, recv, {"sp": me_sp ^ 4})
 
     def gw_part(r):
         parts[r] = mm(att_t[...], nat[r], NN)
@@ -310,62 +349,66 @@
         @pl.when(core_owns(r))
         def _():
             s1_copy(r).wait_recv()
-            total = parts[r] + g1_in[r].astype(f32)
-            parts[r] = total
-            gy_out[r] = total.astype(bf16)
-
-        @pl.when(core_only(r))
+            for i in range(4):
+                for k in range(4):
+                    rows = slice((4 * i + k) * piece, (4 * i + k + 1) * piece)
+                    total = parts[r, rows, :] + g1_in[r, rows, :].astype(f32)
+                    parts[r, rows, :] = total
+                    gy_out[r, i, k] = total.astype(bf16)
+            for j in range(1, 4):
+                gy_copy(r, j).start()
+
+    def gw_sy(r):
+        @pl.when(core_owns(r))
         def _():
-            gy_over(r, 0).start()
-            gy_over(r, 1).start()
+            all_of(gy_in.at[r], r_["gys"].at[0], r_["gyr"].at[r]).wait_recv()
+            for k in range(4):
+                at = pl.multiple_of(y * (4 * piece) + k * piece, 8)
+                total = parts[r, pl.ds(at, piece), :]
+                for j in range(3):
+                    total = total + gy_in[r, j, k].astype(f32)
+                parts[r, k * piece : (k + 1) * piece, :] = total
+                gx_out[r, k] = total.astype(bf16)
+            for j in range(1, 4):
+                gx_copy(r, j).start()
+
+    def gw_sx(r):
+        @pl.when(core_owns(r))
+        def _():
+            all_of(gx_in.at[r], r_["gxs"].at[0], r_["gxr"].at[r]).wait_recv()
+            total = parts[r, pl.ds(pl.multiple_of(x * piece, 8), piece), :]
+            for j in range(3):
+                total = total + gx_in[r, j].astype(f32)
+            fin_out[r] = total.astype(bf16)
+
+        for i in (0, 1):
+
+            @pl.when(ag1_sends(r, i))
+            def _():
+                ag1_copy(r, i).start()
 
         @pl.when(mine(r))
         def _():
-            gy_across(r).start()
-
-    def gw_sy(r):
-        @pl.when(mine(r))
-        def _():
-            for i in range(3):
-                remote(
-                    gy_out.at[r, pl.ds(0, half)],
-                    gy_in.at[r, i],
-                    r_["gys"].at[r, i],
-                    r_["gyr"].at[r, i],
-                    {"sp": me_sp ^ 4},
-                ).wait_recv()
-            total = parts[r, pl.ds(pl.multiple_of(yh * half, half), half), :]
-            for i in range(3):
-                total = total + gy_in[r, i].astype(f32)
-            parts[r, :half, :] = total
-            gx_out[r] = total.astype(bf16)
-            for j in range(1, 4):
-                gx_copy(r, j).start()
-
-    def gw_sx(r):
-        @pl.when(mine(r))
-        def _():
-            for j in range(1, 4):
-                gx_copy(r, j).wait_recv()
-            total = parts[r, pl.ds(pl.multiple_of(x * piece, piece), piece), :]
-            for j in range(3):
-                total = total + gx_in[r, j].astype(f32)
-            ag_out[r] = total.astype(bf16)
-            gfin[blk(r) & 1, pl.ds(pl.multiple_of(me_sp * piece, piece), piece), :] = total.astype(
-                bf16
-            )
-            for j in range(1, n_sp):
-                ag_copy(r, j).start()
-
-    gw_v = r_["gw_v"]
+            gfin[blk(r) & 1, y, x] = fin_out[r]
 
     def gw_ag(r):
         @pl.when(mine(r))
         def _():
-            for j in range(1, n_sp):
-                ag_copy(r, j).wait_recv()
+            all_of(gx_in.at[0], r_["ag1s"].at[0], r_["ag1r"].at[r]).wait_recv()
+            for j in range(1, 4):
+                ag2_copy(r, j).start()
+
+    gw_v = r_["gw_v"]
+
+    def gw_end(r):
+        @pl.when(mine(r))
+        def _():
+            all_of(gy_in.at[0], r_["ag2s"].at[0], r_["ag2r"].at[r]).wait_recv()
             at = pl.ds(pl.multiple_of((blk(r) & 1) * w, HD), w)
-            gw_v[:, at] = gfin[blk(r) & 1].astype(f32)
+            for i in range(4):
+                for k in range(4):
+                    rows = slice((4 * i + k) * piece, (4 * i + k + 1) * piece)
+                    gw_v[rows, at] = gfin[blk(r) & 1, i, k].astype(f32)
 
     trow = text // n_sp
 
@@ -373,8 +416,8 @@
         return remote(
             tx_out.at[me_sp ^ j],
             tx_in.at[j - 1],
-            r_["txs"].at[j - 1],
-            r_["txr"].at[j - 1],
+            r_["txs"].at[0],
+            r_["txr"].at[0],
             {"sp": me_sp ^ j},
         )
 
@@ -382,8 +425,8 @@
         return remote(
             tg.at[me_sp],
             tg.at[me_sp],
-            r_["tgs"].at[j - 1],
-            r_["tgr"].at[j - 1],
+            r_["tgs"].at[0],
+            r_["tgr"].at[0],
             {"sp": me_sp ^ j},
         )
 
@@ -425,59 +468,45 @@
 
     scale(0)
     z_arrive(0, 0)
-    w_core().wait_recv()
     z_arrive(0, 1)
-    w_y(0).wait_recv()
-    w_y(1).wait_recv()
-    w_fwd().start()
     scale(1)
     scale(7)
-    halo_wait_both([item_k(0), item_v(0)])
+    halo_wait_both(("kv", 0))
     forward(0)
-    w_fwd().wait_recv()
-    ga_add(0, True)
     z_arrive(1, 0)
-    halo_wait_both([item_k(1), item_v(1)])
+    halo_wait_both(("kv", 1))
     forward(1)
-    ga_add(1)
-    ga_add(7)
     z_arrive(1, 1)
     scale(2)
     scale(6)
-    halo_wait_both([item_k(2), item_v(2)])
+    w_core().wait_recv()
+    w_y_all(1).wait_recv()
+    w_fwd().start()
+    halo_wait_both(("kv", 2))
     forward(2)
     halo_start([4 * heads])
     z_arrive(2, 0)
     for r in (0, 1, 7):
         gw_part(r)
+    w_fwd().wait_recv()
+    ga_add(0, True)
+    ga_add(1)
+    ga_add(7)
+    for r in (0, 1, 7):
+        gw_s1(r)
+    z_arrive(2, 1)
+    for r in (2, 6):
+        gw_part(r)
     ga_add(2)
     ga_add(6)
-    for r in (0, 1, 7):
+    for r in (2, 6):
         gw_s1(r)
-    for r in (2, 6):
-        gw_part(r)
-    z_arrive(2, 1)
     scale(3)
     scale(5)
+    ga_add(3)
+    ga_add(5)
     for r in (3, 5):
         gw_part(r)
-    for r in (2, 6):
-        gw_s1(r)
-    ga_add(3)
-    ga_add(5)
-    for r in (0, 1, 7):
-        gw_sy(r)
-    halo_wait_both([4 * heads])
-    for h in range(heads):
-        halo_wait_both([item_q(h)])
-        for side in (0, 1):
-            pl.when(has[side])(functools.partial(far_weights, side, h))
-    for r in (3, 5):
-        gw_s1(r)
-    for r in (2, 6):
-        gw_sy(r)
-    for r in (0, 1, 7):
-        gw_sx(r)
     z_arrive(3, 0)
     z_arrive(3, 1)
     scale(4)
@@ -488,58 +517,69 @@
         dl_out[h : h + 1, :] = jnp.sum(
             ga_t[c, :].astype(f32) * att_t[c, :].astype(f32), axis=0, keepdims=True
         )
-    gw_part(4)
     for h in range(heads):
         text_part(h)
     for j in range(1, n_sp):
         tx_copy(j).start()
-    halo_start([4 * heads + 1] + [3 * heads + h for h in range(heads)])
+    for r in (3, 5):
+        gw_s1(r)
+    gw_part(4)
+    for r in (0, 1, 7):
+        gw_sy(r)
+    halo_start([4 * heads + 1, 3 * heads])
+    for r in (2, 6):
+        gw_sy(r)
     gw_s1(4)
+    halo_start([3 * heads + h for h in range(1, heads)])
+    for r in (0, 1, 7):
+        gw_sx(r)
     own_part(0)
     for r in (3, 5):
         gw_sy(r)
     for r in (2, 6):
         gw_sx(r)
     own_part(1)
+    for r in (0, 1, 7):
+        gw_ag(r)
     gw_sy(4)
-    for r in (3, 5):
-        gw_sx(r)
     own_part(2)
     gq_store = pltpu.make_async_copy(gq_v, r_["gq_out"], r_["os"].at[0])
     gq_store.start()
-    for j in range(1, n_sp):
-        tx_copy(j).wait_recv()
+    halo_wait_both(("st", 0), ("q", 0))
+    for h in range(heads):
+        for side in (0, 1):
+            pl.when(has[side])(functools.partial(far_weights, side, h))
+    all_of(tx_in, r_["txs"].at[0], r_["txr"].at[0]).wait_recv()
     total = tx_out[me_sp].astype(f32)
     for j in range(n_sp - 1):
         total = total + tx_in[j].astype(f32)
     tg[me_sp] = total.astype(bf16)
     for j in range(1, n_sp):
         tg_copy(j).start()
+    for r in (3, 5):
+        gw_sx(r)
+    for r in (2, 6):
+        gw_ag(r)
     gw_sx(4)
-    for r in (0, 1, 7, 2, 6, 3, 5):
-        gw_ag(r)
-    halo_wait_both([4 * heads + 1])
+    halo_wait_both(("dl", 0))
     for h in range(heads):
-        halo_wait_both([3 * heads + h])
+        halo_wait_both(("ga", h))
         for side in (0, 1):
             pl.when(has[side])(functools.partial(far_part, side, h))
         c = cols(h)
         gk_v[:, c] = (factor * gk_sum[:, c]).astype(bf16)
         gv_v[:, c] = gv_sum[:, c].astype(bf16)
+        if h == 0:
+            for r in (3, 5):
+                gw_ag(r)
     stored = [
         pltpu.make_async_copy(gk_v, r_["gk_out"], r_["os"].at[1]),
         pltpu.make_async_copy(gv_v, r_["gv_out"], r_["os"].at[2]),
     ]
     for c in stored:
         c.start()
-    for j in range(1, n_sp):
-        remote(
-            tg.at[me_sp],
-            tg.at[me_sp ^ j],
-            r_["tgs"].at[j - 1],
-            r_["tgr"].at[j - 1],
-            {"sp": me_sp ^ j},
-        ).wait_recv()
+    gw_ag(4)
+    all_of(tg.at[pl.ds(0, n_sp - 1)], r_["tgs"].at[0], r_["tgr"].at[0]).wait_recv()
     for j in range(n_sp):
         rows = slice(j * trow, (j + 1) * trow)
         gtk_v[rows] = tg[j, :trow]
@@ -550,48 +590,44 @@
     ]
     for c in late:
         c.start()
-    gw_ag(4)
+    for r in (0, 1, 7, 2, 6, 3, 5, 4):
+        gw_end(r)
     gw_store = pltpu.make_async_copy(gw_v, r_["gw_out"], r_["os"].at[5])
     gw_store.start()
 
-    for up in (True, False):
-        for t in range(4):
-            for c in (0, 1):
-                if z_exists(up, t, c):
-                    z_copy(up, t, c).wait_send()
+    all_of(raw.at[pl.ds(0, n_tp - 1)], r_["zs"].at[0], r_["zr"].at[0, 0, 0]).wait_send()
     w_core().wait_send()
-    w_y(0).wait_send()
-    w_y(1).wait_send()
+
+    @pl.when(jnp.logical_not(ends))
+    def _():
+        w_y_all(1).wait_send()
+
+    @pl.when(ends & gives)
+    def _():
+        w_y_all(2).wait_send()
+
     w_fwd().wait_send()
     for side in (0, 1):
 
         @pl.when(has[side])
         def _():
-            for item in range(4 * heads + 2):
-                halo(side, item).wait_send()
-
-    for r in range(n_tp):
-
-        @pl.when(jnp.logical_not(core_owns(r)))
-        def _():
-            s1_copy(r).wait_send()
-
-        @pl.when(core_only(r))
-        def _():
-            gy_over(r, 0).wait_send()
-            gy_over(r, 1).wait_send()
-
-        @pl.when(mine(r))
-        def _():
-            gy_across(r).wait_send()
-            for j in range(1, 4):
-                gx_copy(r, j).wait_send()
-            for j in range(1, n_sp):
-                ag_copy(r, j).wait_send()
-
-    for j in range(1, n_sp):
-        tx_copy(j).wait_send()
-        tg_copy(j).wait_send()
+            blocks = raw.at[pl.ds(0, 4)]
+            remote(
+                blocks, blocks, r_["hs"].at[side, 0], r_["hr"].at[side, 0], {"sp": side_sp[side]}
+            ).wait_send()
+            halo(side, 4 * heads).wait_send()
+            halo(side, 4 * heads + 1).wait_send()
+
+    for some, n in (
+        (g1_out.at[pl.ds(0, 4)], "s1"),
+        (gy_in.at[pl.ds(0, 4)], "gy"),
+        (gx_in.at[pl.ds(0, 4)], "gx"),
+        (gx_in.at[pl.ds(0, 2)], "ag1"),
+        (gy_in.at[pl.ds(0, 2)], "ag2"),
+        (tx_in, "tx"),
+        (tg.at[pl.ds(0, n_sp - 1)], "tg"),
+    ):
+        all_of(some, r_[n + "s"].at[0], r_[n + "r"].at[0]).wait_send()
     for c in [gq_store] + stored + late + [gw_store]:
         c.wait()
 
@@ -603,7 +639,7 @@
     cols = w.shape[1]
     total = 3 * tok + text
     block = s.shape[1]
-    piece, half = width // 8, width // 2
+    piece = width // 16
     sm = pl.BlockSpec(memory_space=pltpu.SMEM)
     vm = pl.BlockSpec(memory_space=pltpu.VMEM)
     outs = [
@@ -638,36 +674,37 @@
         ("parts", (8, width, block), f32),
         ("g1_out", (8, width, block), bf16),
         ("g1_in", (8, width, block), bf16),
-        ("gy_out", (8, width, block), bf16),
-        ("gy_in", (8, 3, half, block), bf16),
-        ("gx_out", (8, half, block), bf16),
+        ("gy_out", (8, 4, 4, piece, block), bf16),
+        ("gy_in", (8, 3, 4, piece, block), bf16),
+        ("gx_out", (8, 4, piece, block), bf16),
         ("gx_in", (8, 3, piece, block), bf16),
-        ("ag_out", (8, piece, block), bf16),
-        ("gfin", (2, width, block), bf16),
+        ("fin_out", (8, piece, block), bf16),
+        ("gfin", (2, 4, 4, piece, block), bf16),
         ("tx_out", (8, text // 4, width), bf16),
         ("tx_in", (7, text // 4, width), bf16),
         ("tg", (8, text // 4, width), bf16),
     ]
-    items = 4 * heads + 2
     sems = [
-        ("zs", (2, 4, 2)),
+        ("zs", (1,)),
         ("zr", (2, 4, 2)),
-        ("ws", (4,)),
-        ("wr", (4,)),
-        ("hs", (2, items)),
-        ("hr", (2, items)),
-        ("s1s", (8,)),
+        ("ws", (3,)),
+        ("wr", (3,)),
+        ("hs", (2, 3)),
+        ("hr", (2, 2 * heads + 3)),
+        ("s1s", (1,)),
         ("s1r", (8,)),
-        ("gys", (8, 3)),
-        ("gyr", (8, 3)),
-        ("gxs", (8, 3)),
-        ("gxr", (8, 3)),
-        ("ags", (8, 7)),
-        ("agr", (8, 7)),
-        ("txs", (7,)),
-        ("txr", (7,)),
-        ("tgs", (7,)),
-        ("tgr", (7,)),
+        ("gys", (1,)),
+        ("gyr", (8,)),
+        ("gxs", (1,)),
+        ("gxr", (8,)),
+        ("ag1s", (1,)),
+        ("ag1r", (8,)),
+        ("ag2s", (1,)),
+        ("ag2r", (8,)),
+        ("txs", (1,)),
+        ("txr", (1,)),
+        ("tgs", (1,)),
+        ("tgr", (1,)),
         ("os", (6,)),
     ]
     args = ["q", "k", "v", "tk", "tv", "s", "w", "gate", "win", "map", "live"]
@@ -676,7 +713,7 @@
     return pl.pallas_call(
         functools.partial(kernel, tuple(names)),
         out_shape=[jax.ShapeDtypeStruct(a, b) for _, a, b in outs],
-        in_specs=[vm] * 9 + [sm] * 2,
+        in_specs=[vm] * 10 + [sm],
         out_specs=[pl.BlockSpec(memory_space=pl.ANY)] * len(outs),
         scratch_shapes=[pltpu.VMEM(a, b) for _, a, b in scratch]
         + [pltpu.SemaphoreType.DMA(n) for _, n in sems],
@@ -739,7 +776,7 @@
         out_weight,
         gate,
         windows,
-        tile_map,
+        tile_map.T,
         text_count,
     )
     outs = copy_call(outs)

time: 108 us -> 81.7 us (0.76); the launches traced: 107 us -> 81.5 us
  Pallas kernels: 104 us -> 80.1 us
  local copies, waits for them, and re-layouts: 1.32 us -> 0 us
    pallas_call x1, Pallas kernels: 101 us -> 77.3 us  [call(): pl.pallas_call(functools.partial(kernel, tuple(names)), out_shape=[jax.Sh...]
    unnamed x1 -> x0, local copies, waits for them, and re-layouts: 1.32 us -> none
where the time goes in v1:
time: 81.7 us; the launch traced here: 81.5 us
  Pallas kernels  80.1 us (98%)
  between operations  1.45 us (2%)
    pallas_call x1, Pallas kernels, call(): pl.pallas_call(functools.partial(kernel, tuple(names)), out_shape=[jax.Sh...  77.3 us
    pallas_call x1, Pallas kernels, copy_call(): pl.pallas_call(functools.partial(copy_kernel, n), out_shape=[jax.ShapeDty...  2.79 us

profile of v1, /device:TPU:8, one launch (start us, length us, event | category | flops | bytes accessed | tf_op | source)
XLA Modules:
  0.0 81.5 jit_solution(11482193582459561867)
XLA Ops:
  1.3 77.3 %attention_backward.1 = (bf16[384,384]{1,0:T(8,128)(2,1)}, bf16[384,384]{1,0:T(8,128)(2,1)}, bf16[384,384]{1,0:T(8,128)(2,1)}, bf16[256,384]{1,0:T(8,128)(2,1)},...) custom-call(bf16[384,384]{1,0:T(8,128)(2,1)} %bitcast.12, bf16[384,384]{1,0:T(8,128)(2,1)} %bitcast.13, ...), custom_call_target="tpu_custom_call" | custom-call | tf_op jit(solution)/shard_map/attention_backward/pallas_call | solution.py:713
  78.6 2.8 %results.1 = (bf16[384,384]{1,0:T(8,128)(2,1)}, bf16[384,384]{1,0:T(8,128)(2,1)}, bf16[384,384]{1,0:T(8,128)(2,1)}, bf16[256,384]{1,0:T(8,128)(2,1)}, bf16[256,384]{1,0:T(8,128)(2,1)}, /*index=5*/f32[384,768]{1,0:T(8,128)}) custom-call(bf16[384,384]{1,0:T(8,128)(2,1)} %get-tuple-element.18.refs_0_, bf16[384,384]{1,0:T(8,128)(2,1)} %get-tuple-element.19.refs_1_, ...), custom_call_target="tpu_custom_call" | custom-call | tf_op jit(solution)/shard_map/results/pallas_call | solution.py:744

commit v2 on v1

--- a/solution.py
+++ b/solution.py
@@ -48,7 +48,7 @@
     ga_t, att_t, wts, wfar, gs_buf = r_["ga_t"], r_["att_t"], r_["wts"], r_["wfar"], r_["gs_buf"]
     parts, g1_out, g1_in = r_["parts"], r_["g1_out"], r_["g1_in"]
     gy_out, gy_in, gx_out, gx_in = r_["gy_out"], r_["gy_in"], r_["gx_out"], r_["gx_in"]
-    fin_out, gfin = r_["fin_out"], r_["gfin"]
+    gall, gfin = r_["gall"], r_["gfin"]
     tx_out, tx_in, tg = r_["tx_out"], r_["tx_in"], r_["tg"]
     gk_sum, gv_sum = r_["gk_sum"], r_["gv_sum"]
 
@@ -107,8 +107,9 @@
     def z_exists(up, t, c):
         return t < 3 or (t == 3 and c == (0 if up else 1))
 
-    def z_arrive(t, c):
+    def z_arrive(t, i):
         for up in (True, False):
+            c = i if up else 1 - i
             if z_exists(up, t, c):
                 z_copy(up, t, c).wait_recv()
                 if t < 3 and z_exists(up, t + 1, c):
@@ -193,7 +194,7 @@
 
     for c in (0, 1):
         z_copy(True, 0, c).start()
-        z_copy(False, 0, c).start()
+        z_copy(False, 0, 1 - c).start()
     w_core().start()
 
     @pl.when(jnp.logical_not(ends))
@@ -297,10 +298,25 @@
             g1_out.at[r], g1_in.at[r], r_["s1s"].at[0], r_["s1r"].at[r], {"dp": me_dp ^ 1}
         )
 
+    def x_first(r):
+        return r in (2, 6)
+
+    def along_x(j):
+        return {"sp": me_sp ^ j}
+
+    def along_y(j):
+        return {"dp": me_dp ^ (2 * (j & 1)), "sp": me_sp ^ (2 * (j & 2))}
+
+    def place1(r):
+        return x if x_first(r) else y
+
+    def place2(r):
+        return y if x_first(r) else x
+
     def gy_copy(r, j):
-        where = {"dp": me_dp ^ (2 * (j & 1)), "sp": me_sp ^ (2 * (j & 2))}
+        where = along_x(j) if x_first(r) else along_y(j)
         return remote(
-            gy_out.at[r, y ^ j],
+            gy_out.at[r, place1(r) ^ j],
             gy_in.at[r, j - 1],
             r_["gys"].at[0],
             r_["gyr"].at[r],
@@ -308,31 +324,30 @@
         )
 
     def gx_copy(r, j):
+        where = along_y(j) if x_first(r) else along_x(j)
         return remote(
-            gx_out.at[r, x ^ j],
+            gx_out.at[r, place2(r) ^ j],
             gx_in.at[r, j - 1],
             r_["gxs"].at[0],
             r_["gxr"].at[r],
-            {"sp": me_sp ^ j},
-        )
-
-    def ag1_copy(r, i):
+            where,
+        )
+
+    def ag1_copy(r, j):
+        piece_ = gall.at[r, x]
+        return remote(piece_, piece_, r_["ag1s"].at[0], r_["ag1r"].at[r], along_x(j))
+
+    def ag2_copy(r, i):
         return remote(
-            fin_out.at[r],
-            gfin.at[blk(r) & 1, y, x],
-            r_["ag1s"].at[0],
-            r_["ag1r"].at[r],
+            gall.at[r],
+            gfin.at[blk(r) & 1, y],
+            r_["ag2s"].at[0],
+            r_["ag2r"].at[r],
             {"dp": blk(r) >> 1, "sp": 4 * i + x},
         )
 
-    def ag1_sends(r, i):
+    def ag2_sends(r, i):
         return core_owns(r) & jnp.logical_not(mine(r) & (yh == i))
-
-    def ag2_copy(r, j):
-        slab = gfin.at[blk(r) & 1, :, x]
-        return remote(
-            slab, slab, r_["ag2s"].at[0], r_["ag2r"].at[r], {"sp": me_sp ^ j}
-        )
 
     def all_of(some, send, recv):
         return remote(some, some, send, recv, {"sp": me_sp ^ 4})
@@ -363,7 +378,7 @@
         def _():
             all_of(gy_in.at[r], r_["gys"].at[0], r_["gyr"].at[r]).wait_recv()
             for k in range(4):
-                at = pl.multiple_of(y * (4 * piece) + k * piece, 8)
+                at = pl.multiple_of(place1(r) * (4 * piece) + k * piece, 8)
                 total = parts[r, pl.ds(at, piece), :]
                 for j in range(3):
                     total = total + gy_in[r, j, k].astype(f32)
@@ -376,27 +391,27 @@
         @pl.when(core_owns(r))
         def _():
             all_of(gx_in.at[r], r_["gxs"].at[0], r_["gxr"].at[r]).wait_recv()
-            total = parts[r, pl.ds(pl.multiple_of(x * piece, 8), piece), :]
+            total = parts[r, pl.ds(pl.multiple_of(place2(r) * piece, 8), piece), :]
             for j in range(3):
                 total = total + gx_in[r, j].astype(f32)
-            fin_out[r] = total.astype(bf16)
+            gall[r, x] = total.astype(bf16)
+            for j in range(1, 4):
+                ag1_copy(r, j).start()
+
+    def gw_ag(r):
+        @pl.when(core_owns(r))
+        def _():
+            all_of(gx_in.at[0], r_["ag1s"].at[0], r_["ag1r"].at[r]).wait_recv()
 
         for i in (0, 1):
 
-            @pl.when(ag1_sends(r, i))
+            @pl.when(ag2_sends(r, i))
             def _():
-                ag1_copy(r, i).start()
+                ag2_copy(r, i).start()
 
         @pl.when(mine(r))
         def _():
-            gfin[blk(r) & 1, y, x] = fin_out[r]
-
-    def gw_ag(r):
-        @pl.when(mine(r))
-        def _():
-            all_of(gx_in.at[0], r_["ag1s"].at[0], r_["ag1r"].at[r]).wait_recv()
-            for j in range(1, 4):
-                ag2_copy(r, j).start()
+            gfin[blk(r) & 1, y] = gall[r]
 
     gw_v = r_["gw_v"]
 
@@ -407,7 +422,8 @@
             at = pl.ds(pl.multiple_of((blk(r) & 1) * w, HD), w)
             for i in range(4):
                 for k in range(4):
-                    rows = slice((4 * i + k) * piece, (4 * i + k + 1) * piece)
+                    n = 4 * k + i if x_first(r) else 4 * i + k
+                    rows = slice(n * piece, (n + 1) * piece)
                     gw_v[rows, at] = gfin[blk(r) & 1, i, k].astype(f32)
 
     trow = text // n_sp
@@ -485,31 +501,31 @@
     halo_wait_both(("kv", 2))
     forward(2)
     halo_start([4 * heads])
-    z_arrive(2, 0)
     for r in (0, 1, 7):
         gw_part(r)
+    z_arrive(2, 0)
     w_fwd().wait_recv()
     ga_add(0, True)
     ga_add(1)
     ga_add(7)
     for r in (0, 1, 7):
         gw_s1(r)
-    z_arrive(2, 1)
     for r in (2, 6):
         gw_part(r)
     ga_add(2)
     ga_add(6)
-    for r in (2, 6):
-        gw_s1(r)
+    z_arrive(2, 1)
     scale(3)
     scale(5)
     ga_add(3)
     ga_add(5)
     for r in (3, 5):
         gw_part(r)
+    for r in (2, 6):
+        gw_s1(r)
     z_arrive(3, 0)
-    z_arrive(3, 1)
     scale(4)
+    gw_part(4)
     ga_add(4)
     ga_t[...] = acc[...].astype(bf16)
     for h in range(heads):
@@ -517,30 +533,25 @@
         dl_out[h : h + 1, :] = jnp.sum(
             ga_t[c, :].astype(f32) * att_t[c, :].astype(f32), axis=0, keepdims=True
         )
+    for r in (3, 5):
+        gw_s1(r)
     for h in range(heads):
         text_part(h)
+    gw_s1(4)
+    for r in (0, 1, 7):
+        gw_sy(r)
     for j in range(1, n_sp):
         tx_copy(j).start()
-    for r in (3, 5):
-        gw_s1(r)
-    gw_part(4)
-    for r in (0, 1, 7):
+    for r in (2, 6):
         gw_sy(r)
     halo_start([4 * heads + 1, 3 * heads])
-    for r in (2, 6):
-        gw_sy(r)
-    gw_s1(4)
-    halo_start([3 * heads + h for h in range(1, heads)])
+    own_part(0)
     for r in (0, 1, 7):
         gw_sx(r)
-    own_part(0)
     for r in (3, 5):
         gw_sy(r)
-    for r in (2, 6):
-        gw_sx(r)
+    halo_start([3 * heads + h for h in range(1, heads)])
     own_part(1)
-    for r in (0, 1, 7):
-        gw_ag(r)
     gw_sy(4)
     own_part(2)
     gq_store = pltpu.make_async_copy(gq_v, r_["gq_out"], r_["os"].at[0])
@@ -549,15 +560,19 @@
     for h in range(heads):
         for side in (0, 1):
             pl.when(has[side])(functools.partial(far_weights, side, h))
+    for r in (2, 6):
+        gw_sx(r)
+    for r in (0, 1, 7):
+        gw_ag(r)
     all_of(tx_in, r_["txs"].at[0], r_["txr"].at[0]).wait_recv()
     total = tx_out[me_sp].astype(f32)
     for j in range(n_sp - 1):
         total = total + tx_in[j].astype(f32)
     tg[me_sp] = total.astype(bf16)
+    for r in (3, 5):
+        gw_sx(r)
     for j in range(1, n_sp):
         tg_copy(j).start()
-    for r in (3, 5):
-        gw_sx(r)
     for r in (2, 6):
         gw_ag(r)
     gw_sx(4)
@@ -572,13 +587,14 @@
         if h == 0:
             for r in (3, 5):
                 gw_ag(r)
+        if h == 1:
+            gw_ag(4)
     stored = [
         pltpu.make_async_copy(gk_v, r_["gk_out"], r_["os"].at[1]),
         pltpu.make_async_copy(gv_v, r_["gv_out"], r_["os"].at[2]),
     ]
     for c in stored:
         c.start()
-    gw_ag(4)
     all_of(tg.at[pl.ds(0, n_sp - 1)], r_["tgs"].at[0], r_["tgr"].at[0]).wait_recv()
     for j in range(n_sp):
         rows = slice(j * trow, (j + 1) * trow)
@@ -622,7 +638,7 @@
         (g1_out.at[pl.ds(0, 4)], "s1"),
         (gy_in.at[pl.ds(0, 4)], "gy"),
         (gx_in.at[pl.ds(0, 4)], "gx"),
-        (gx_in.at[pl.ds(0, 2)], "ag1"),
+        (gx_in.at[pl.ds(0, 4)], "ag1"),
         (gy_in.at[pl.ds(0, 2)], "ag2"),
         (tx_in, "tx"),
         (tg.at[pl.ds(0, n_sp - 1)], "tg"),
@@ -678,7 +694,7 @@
         ("gy_in", (8, 3, 4, piece, block), bf16),
         ("gx_out", (8, 4, piece, block), bf16),
         ("gx_in", (8, 3, piece, block), bf16),
-        ("fin_out", (8, piece, block), bf16),
+        ("gall", (8, 4, piece, block), bf16),
         ("gfin", (2, 4, 4, piece, block), bf16),
         ("tx_out", (8, text // 4, width), bf16),
         ("tx_in", (7, text // 4, width), bf16),

time: 81.7 us -> 72.1 us (0.88)
  Pallas kernels: 80.1 us -> 70.3 us
    pallas_call x1, Pallas kernels: 77.3 us -> 67.5 us  [call(): pl.pallas_call(functools.partial(kernel, tuple(names)), out_shape=[jax.Sh...]
where the time goes in v2:
time: 72.1 us; the launch traced here: 71.8 us
  Pallas kernels  70.3 us (98%)
  between operations  1.45 us (2%)
    pallas_call x1, Pallas kernels, call(): pl.pallas_call(functools.partial(kernel, tuple(names)), out_shape=[jax.Sh...  67.5 us
    pallas_call x1, Pallas kernels, copy_call(): pl.pallas_call(functools.partial(copy_kernel, n), out_shape=[jax.ShapeDty...  2.79 us

profile of v2, /device:TPU:8, one launch (start us, length us, event | category | flops | bytes accessed | tf_op | source)
XLA Modules:
  0.0 71.8 jit_solution(17611288634368735440)
XLA Ops:
  1.3 67.5 %attention_backward.1 = (bf16[384,384]{1,0:T(8,128)(2,1)}, bf16[384,384]{1,0:T(8,128)(2,1)}, bf16[384,384]{1,0:T(8,128)(2,1)}, bf16[256,384]{1,0:T(8,128)(2,1)},...) custom-call(bf16[384,384]{1,0:T(8,128)(2,1)} %bitcast.12, bf16[384,384]{1,0:T(8,128)(2,1)} %bitcast.13, ...), custom_call_target="tpu_custom_call" | custom-call | tf_op jit(solution)/shard_map/attention_backward/pallas_call | solution.py:729
  68.8 2.8 %results.1 = (bf16[384,384]{1,0:T(8,128)(2,1)}, bf16[384,384]{1,0:T(8,128)(2,1)}, bf16[384,384]{1,0:T(8,128)(2,1)}, bf16[256,384]{1,0:T(8,128)(2,1)}, bf16[256,384]{1,0:T(8,128)(2,1)}, /*index=5*/f32[384,768]{1,0:T(8,128)}) custom-call(bf16[384,384]{1,0:T(8,128)(2,1)} %get-tuple-element.18.refs_0_, bf16[384,384]{1,0:T(8,128)(2,1)} %get-tuple-element.19.refs_1_, ...), custom_call_target="tpu_custom_call" | custom-call | tf_op jit(solution)/shard_map/results/pallas_call | solution.py:760

commit v3 on v2

--- a/solution.py
+++ b/solution.py
@@ -39,8 +39,7 @@
     *refs,
 ):
     r_ = dict(zip(names, refs, strict=True))
-    q_ref, k_ref, v_ref, tk_ref, tv_ref = (r_[n] for n in ("q", "k", "v", "tk", "tv"))
-    s_ref, w_ref, gate_ref, win_ref = (r_[n] for n in ("s", "w", "gate", "win"))
+    q_ref, s_ref, gate_ref, win_ref = (r_[n] for n in ("q_v", "s_v", "gate", "win"))
     map_ref, live_ref = r_["map"], r_["live"]
     keys, vals, qf, gaf = r_["keys"], r_["vals"], r_["qf"], r_["gaf"]
     st_out, st_in, dl_out, dl_in = r_["st_out"], r_["st_in"], r_["dl_out"], r_["dl_in"]
@@ -50,11 +49,12 @@
     gy_out, gy_in, gx_out, gx_in = r_["gy_out"], r_["gy_in"], r_["gx_out"], r_["gx_in"]
     gall, gfin = r_["gall"], r_["gfin"]
     tx_out, tx_in, tg = r_["tx_out"], r_["tx_in"], r_["tg"]
+    ty_out, ty_in, t_own = r_["ty_out"], r_["ty_in"], r_["t_own"]
     gk_sum, gv_sum = r_["gk_sum"], r_["gv_sum"]
 
     factor = HD ** (-0.5)
     tok, width = q_ref.shape
-    text = tk_ref.shape[0]
+    text = r_["tk"].shape[0]
     heads = width // HD
     near = tok + text
     n_tp = n_sp = 8
@@ -78,6 +78,24 @@
     barrier = pltpu.get_barrier_semaphore()
     for where in partners:
         pl.semaphore_signal(barrier, inc=1, device_id=where, device_id_type=MESH)
+
+    w_ref = w_all.at[me_dp]
+    loads = {
+        n: pltpu.make_async_copy(r_[n], to, r_["ls"].at[i])
+        for i, (n, to) in enumerate(
+            [
+                ("s", s_ref),
+                ("w", w_ref),
+                ("k", keys.at[pl.ds(0, tok)]),
+                ("v", vals.at[pl.ds(0, tok)]),
+                ("q", q_ref),
+                ("tk", keys.at[pl.ds(tok, text)]),
+                ("tv", vals.at[pl.ds(tok, text)]),
+            ]
+        )
+    }
+    for c in loads.values():
+        c.start()
     pl.semaphore_wait(barrier, len(partners))
 
     def remote(src, dst, send, recv, where):
@@ -146,7 +164,7 @@
         if item < 3 * heads:
             h, kind = divmod(item, 3)
             c = pl.ds(h * HD, HD)
-            src = (k_ref, v_ref, q_ref)[kind].at[:, c]
+            src = (keys.at[pl.ds(0, tok), c], vals.at[pl.ds(0, tok), c], q_ref.at[:, c])[kind]
             dst = (keys.at[region, c], vals.at[region, c], qf.at[there, :, c])[kind]
         elif item < 4 * heads:
             c = pl.ds((item - 3 * heads) * HD, HD)
@@ -192,9 +210,11 @@
                 for what in whats:
                     halo_wait(side, what)
 
+    loads["s"].wait()
     for c in (0, 1):
         z_copy(True, 0, c).start()
         z_copy(False, 0, 1 - c).start()
+    loads["w"].wait()
     w_core().start()
 
     @pl.when(jnp.logical_not(ends))
@@ -208,16 +228,15 @@
             for j in (0, 1):
                 w_y(i, j).start()
 
+    loads["k"].wait()
+    loads["v"].wait()
     for h in range(heads):
         halo_start([item_k(h), item_v(h)])
+    loads["q"].wait()
     for h in range(heads):
         halo_start([item_q(h)])
-
-    keys[:tok] = k_ref[...]
-    keys[tok:near] = tk_ref[...]
-    vals[:tok] = v_ref[...]
-    vals[tok:near] = tv_ref[...]
-    w_all[me_dp] = w_ref[...]
+    loads["tk"].wait()
+    loads["tv"].wait()
     for side in (0, 1):
 
         @pl.when(jnp.logical_not(has[side]))
@@ -430,21 +449,49 @@
 
     def tx_copy(j):
         return remote(
-            tx_out.at[me_sp ^ j],
-            tx_in.at[j - 1],
-            r_["txs"].at[0],
-            r_["txr"].at[0],
-            {"sp": me_sp ^ j},
-        )
-
-    def tg_copy(j):
-        return remote(
-            tg.at[me_sp],
-            tg.at[me_sp],
-            r_["tgs"].at[0],
-            r_["tgr"].at[0],
-            {"sp": me_sp ^ j},
-        )
+            tx_out.at[x ^ j], tx_in.at[j - 1], r_["txs"].at[0], r_["txr"].at[0], along_x(j)
+        )
+
+    def ty_copy():
+        return remote(ty_out, ty_in, r_["tys"].at[0], r_["tyr"].at[0], {"sp": me_sp ^ 4})
+
+    def tg_copy():
+        slot = tg.at[x, yh]
+        return remote(slot, slot, r_["tgs"].at[0], r_["tgr"].at[0], {"sp": me_sp ^ 4})
+
+    def tz_copy(j):
+        return remote(tg.at[x], tg.at[x], r_["tzs"].at[0], r_["tzr"].at[0], along_x(j))
+
+    def text_1():
+        all_of(tx_in, r_["txs"].at[0], r_["txr"].at[0]).wait_recv()
+
+        def over_x(i):
+            total = tx_out[x, i].astype(f32)
+            for j in range(3):
+                total = total + tx_in[j, i].astype(f32)
+            return total
+
+        ty_out[...] = over_x(1 - yh).astype(bf16)
+        ty_copy().start()
+        t_own[...] = over_x(yh)
+
+    def text_2():
+        ty_copy().wait_recv()
+        tg[x, yh] = (t_own[...] + ty_in[...].astype(f32)).astype(bf16)
+        tg_copy().start()
+
+    def text_3():
+        tg_copy().wait_recv()
+        for j in range(1, 4):
+            tz_copy(j).start()
+
+    def text_4():
+        all_of(tx_in, r_["tzs"].at[0], r_["tzr"].at[0]).wait_recv()
+        for i in range(4):
+            for k in range(2):
+                rows = slice((2 * i + k) * trow, (2 * i + k + 1) * trow)
+                gtk_v[rows] = tg[i, k, :trow]
+                gtv_v[rows] = tg[i, k, trow:]
 
     gq_v, gk_v, gv_v, gtk_v, gtv_v = (r_[n] for n in ("gq_v", "gk_v", "gv_v", "gtk_v", "gtv_v"))
 
@@ -459,8 +506,8 @@
         gv = mm(wt.astype(bf16), ga, NT).astype(bf16)
         for j in range(n_sp):
             rows = slice(j * trow, (j + 1) * trow)
-            tx_out[j, :trow, c] = gk[rows]
-            tx_out[j, trow:, c] = gv[rows]
+            tx_out[j // 2, j % 2, :trow, c] = gk[rows]
+            tx_out[j // 2, j % 2, trow:, c] = gv[rows]
 
     def own_part(h):
         c = cols(h)
@@ -504,17 +551,18 @@
     for r in (0, 1, 7):
         gw_part(r)
     z_arrive(2, 0)
+    gw_s1(0)
+    gw_s1(1)
     w_fwd().wait_recv()
     ga_add(0, True)
+    gw_s1(7)
+    for r in (2, 6):
+        gw_part(r)
     ga_add(1)
     ga_add(7)
-    for r in (0, 1, 7):
-        gw_s1(r)
-    for r in (2, 6):
-        gw_part(r)
     ga_add(2)
+    z_arrive(2, 1)
     ga_add(6)
-    z_arrive(2, 1)
     scale(3)
     scale(5)
     ga_add(3)
@@ -540,7 +588,7 @@
     gw_s1(4)
     for r in (0, 1, 7):
         gw_sy(r)
-    for j in range(1, n_sp):
+    for j in range(1, 4):
         tx_copy(j).start()
     for r in (2, 6):
         gw_sy(r)
@@ -550,12 +598,12 @@
         gw_sx(r)
     for r in (3, 5):
         gw_sy(r)
-    halo_start([3 * heads + h for h in range(1, heads)])
+    halo_start([3 * heads + 1])
     own_part(1)
     gw_sy(4)
+    halo_start([3 * heads + 2])
     own_part(2)
-    gq_store = pltpu.make_async_copy(gq_v, r_["gq_out"], r_["os"].at[0])
-    gq_store.start()
+    text_1()
     halo_wait_both(("st", 0), ("q", 0))
     for h in range(heads):
         for side in (0, 1):
@@ -564,52 +612,32 @@
         gw_sx(r)
     for r in (0, 1, 7):
         gw_ag(r)
-    all_of(tx_in, r_["txs"].at[0], r_["txr"].at[0]).wait_recv()
-    total = tx_out[me_sp].astype(f32)
-    for j in range(n_sp - 1):
-        total = total + tx_in[j].astype(f32)
-    tg[me_sp] = total.astype(bf16)
+    text_2()
     for r in (3, 5):
         gw_sx(r)
-    for j in range(1, n_sp):
-        tg_copy(j).start()
-    for r in (2, 6):
-        gw_ag(r)
-    gw_sx(4)
-    halo_wait_both(("dl", 0))
-    for h in range(heads):
+
+    def far_head(h):
         halo_wait_both(("ga", h))
         for side in (0, 1):
             pl.when(has[side])(functools.partial(far_part, side, h))
         c = cols(h)
         gk_v[:, c] = (factor * gk_sum[:, c]).astype(bf16)
         gv_v[:, c] = gv_sum[:, c].astype(bf16)
-        if h == 0:
-            for r in (3, 5):
-                gw_ag(r)
-        if h == 1:
-            gw_ag(4)
-    stored = [
-        pltpu.make_async_copy(gk_v, r_["gk_out"], r_["os"].at[1]),
-        pltpu.make_async_copy(gv_v, r_["gv_out"], r_["os"].at[2]),
-    ]
-    for c in stored:
-        c.start()
-    all_of(tg.at[pl.ds(0, n_sp - 1)], r_["tgs"].at[0], r_["tgr"].at[0]).wait_recv()
-    for j in range(n_sp):
-        rows = slice(j * trow, (j + 1) * trow)
-        gtk_v[rows] = tg[j, :trow]
-        gtv_v[rows] = tg[j, trow:]
-    late = [
-        pltpu.make_async_copy(gtk_v, r_["gtk_out"], r_["os"].at[3]),
-        pltpu.make_async_copy(gtv_v, r_["gtv_out"], r_["os"].at[4]),
-    ]
-    for c in late:
-        c.start()
+
+    halo_wait_both(("dl", 0))
+    far_head(0)
+    gw_sx(4)
+    for r in (2, 6):
+        gw_ag(r)
+    far_head(1)
+    for r in (3, 5):
+        gw_ag(r)
+    text_3()
+    gw_ag(4)
+    far_head(2)
+    text_4()
     for r in (0, 1, 7, 2, 6, 3, 5, 4):
         gw_end(r)
-    gw_store = pltpu.make_async_copy(gw_v, r_["gw_out"], r_["os"].at[5])
-    gw_store.start()
 
     all_of(raw.at[pl.ds(0, n_tp - 1)], r_["zs"].at[0], r_["zr"].at[0, 0, 0]).wait_send()
     w_core().wait_send()
@@ -641,11 +669,11 @@
         (gx_in.at[pl.ds(0, 4)], "ag1"),
         (gy_in.at[pl.ds(0, 2)], "ag2"),
         (tx_in, "tx"),
-        (tg.at[pl.ds(0, n_sp - 1)], "tg"),
+        (ty_out, "ty"),
+        (ty_out, "tg"),
+        (tx_in, "tz"),
     ):
         all_of(some, r_[n + "s"].at[0], r_[n + "r"].at[0]).wait_send()
-    for c in [gq_store] + stored + late + [gw_store]:
-        c.wait()
 
 
 def call(q, k, v, tk, tv, s, w, gate, windows, tile_map, text_count):
@@ -653,6 +681,7 @@
     text = tk.shape[0]
     heads = width // HD
     cols = w.shape[1]
+    hbm = pl.BlockSpec(memory_space=pltpu.HBM)
     total = 3 * tok + text
     block = s.shape[1]
     piece = width // 16
@@ -666,7 +695,9 @@
         ("gtv", (text, width), bf16),
         ("gw", (width, cols), f32),
     ]
-    scratch = [(n + "_v", a, b) for n, a, b in outs] + [
+    scratch = [
+        ("q_v", (tok, width), bf16),
+        ("s_v", (tok, block), bf16),
         ("keys", (total, width), bf16),
         ("vals", (total, width), bf16),
         ("qf", (2, tok, width), bf16),
@@ -696,9 +727,12 @@
         ("gx_in", (8, 3, piece, block), bf16),
         ("gall", (8, 4, piece, block), bf16),
         ("gfin", (2, 4, 4, piece, block), bf16),
-        ("tx_out", (8, text // 4, width), bf16),
-        ("tx_in", (7, text // 4, width), bf16),
-        ("tg", (8, text // 4, width), bf16),
+        ("tx_out", (4, 2, text // 4, width), bf16),
+        ("tx_in", (3, 2, text // 4, width), bf16),
+        ("ty_out", (text // 4, width), bf16),
+        ("ty_in", (text // 4, width), bf16),
+        ("t_own", (text // 4, width), f32),
+        ("tg", (4, 2, text // 4, width), bf16),
     ]
     sems = [
         ("zs", (1,)),
@@ -719,52 +753,49 @@
         ("ag2r", (8,)),
         ("txs", (1,)),
         ("txr", (1,)),
+        ("tys", (1,)),
+        ("tyr", (1,)),
+        ("tzs", (1,)),
+        ("tzr", (1,)),
         ("tgs", (1,)),
         ("tgr", (1,)),
-        ("os", (6,)),
+        ("ls", (7,)),
     ]
     args = ["q", "k", "v", "tk", "tv", "s", "w", "gate", "win", "map", "live"]
-    names = args + [n + "_out" for n, _, _ in outs] + [n for n, _, _ in scratch]
+    names = args + [n + "_v" for n, _, _ in outs] + [n for n, _, _ in scratch]
     names += [n for n, _ in sems]
     return pl.pallas_call(
         functools.partial(kernel, tuple(names)),
-        out_shape=[jax.ShapeDtypeStruct(a, b) for _, a, b in outs],
-        in_specs=[vm] * 10 + [sm],
-        out_specs=[pl.BlockSpec(memory_space=pl.ANY)] * len(outs),
+        out_shape=[pltpu.VMEM(a, b) for _, a, b in outs],
+        in_specs=[hbm] * 7 + [vm] * 3 + [sm],
+        out_specs=[vm] * len(outs),
         scratch_shapes=[pltpu.VMEM(a, b) for _, a, b in scratch]
         + [pltpu.SemaphoreType.DMA(n) for _, n in sems],
         compiler_params=pltpu.CompilerParams(
-            collective_id=0, has_side_effects=True, vmem_limit_bytes=VMEM
+            collective_id=0, has_side_effects=True, vmem_limit_bytes=56 << 20
         ),
         name="attention_backward",
     )(q, k, v, tk, tv, s, w, gate, windows, tile_map, text_count)
 
 
 def copy_kernel(n, *refs):
-    srcs, dsts, held = refs[:n], refs[n : 2 * n], refs[2 * n : 3 * n]
-    in_sem, out_sem = refs[3 * n :]
-    loads = [pltpu.make_async_copy(srcs[i], held[i], in_sem.at[i]) for i in range(n)]
-    stores = [pltpu.make_async_copy(held[i], dsts[i], out_sem.at[i]) for i in range(n)]
-    for c in loads:
+    srcs, dsts, sem = refs[:n], refs[n : 2 * n], refs[2 * n]
+    stores = [pltpu.make_async_copy(srcs[i], dsts[i], sem.at[i]) for i in range(n)]
+    for c in stores:
         c.start()
-    for i in range(n):
-        loads[i].wait()
-        stores[i].start()
     for c in stores:
         c.wait()
 
 
 def copy_call(arrays):
     n = len(arrays)
-    hbm = pl.BlockSpec(memory_space=pltpu.HBM)
     return pl.pallas_call(
         functools.partial(copy_kernel, n),
         out_shape=[jax.ShapeDtypeStruct(a.shape, a.dtype) for a in arrays],
-        in_specs=[hbm] * n,
-        out_specs=[hbm] * n,
-        scratch_shapes=[pltpu.VMEM(a.shape, a.dtype) for a in arrays]
-        + [pltpu.SemaphoreType.DMA((n,))] * 2,
-        compiler_params=pltpu.CompilerParams(vmem_limit_bytes=VMEM),
+        in_specs=[pl.BlockSpec(memory_space=pltpu.VMEM)] * n,
+        out_specs=[pl.BlockSpec(memory_space=pltpu.HBM)] * n,
+        scratch_shapes=[pltpu.SemaphoreType.DMA((n,))],
+        compiler_params=pltpu.CompilerParams(vmem_limit_bytes=4 << 20),
         name="results",
     )(*arrays)
 

time: 72.1 us -> 67.1 us (0.931); the launches traced: 71.8 us -> 65.9 us
  Pallas kernels: 70.3 us -> 64.5 us
    pallas_call x1, Pallas kernels: 67.5 us -> 63 us  [call(): pl.pallas_call(functools.partial(kernel, tuple(names)), out_shape=[pltpu....]
    pallas_call x1, Pallas kernels: 2.79 us -> 1.49 us  [copy_call(): pl.pallas_call(functools.partial(copy_kernel, n), out_shape=[jax.ShapeDty...]
where the time goes in v3:
time: 67.1 us; the launch traced here: 65.9 us
  Pallas kernels  64.5 us (96%)
  between operations  1.45 us (2%)
    pallas_call x1, Pallas kernels, call(): pl.pallas_call(functools.partial(kernel, tuple(names)), out_shape=[pltpu....  63 us
    pallas_call x1, Pallas kernels, copy_call(): pl.pallas_call(functools.partial(copy_kernel, n), out_shape=[jax.ShapeDty...  1.49 us

profile of v3, /device:TPU:8, one launch (start us, length us, event | category | flops | bytes accessed | tf_op | source)
XLA Modules:
  0.0 65.9 jit_solution(5016362055465554011)
XLA Ops:
  1.3 63.0 %attention_backward.1 = (bf16[384,384]{1,0:T(8,128)(2,1)S(1)}, bf16[384,384]{1,0:T(8,128)(2,1)S(1)}, bf16[384,384]{1,0:T(8,128)(2,1)S(1)}, bf16[256,384]{1,0:T(8...) custom-call(bf16[384,384]{1,0:T(8,128)(2,1)} %bitcast.12, bf16[384,384]{1,0:T(8,128)(2,1)} %bitcast.13, ...), custom_call_target="tpu_custom_call" | custom-call | tf_op jit(solution)/shard_map/attention_backward/pallas_call | solution.py:767
  64.3 1.5 %results.1 = (bf16[384,384]{1,0:T(8,128)(2,1)}, bf16[384,384]{1,0:T(8,128)(2,1)}, bf16[384,384]{1,0:T(8,128)(2,1)}, bf16[256,384]{1,0:T(8,128)(2,1)}, bf16[256,384]{1,0:T(8,128)(2,1)}, /*index=5*/f32[384,768]{1,0:T(8,128)}) custom-call(bf16[384,384]{1,0:T(8,128)(2,1)S(1)} %get-tuple-element.18.refs_0_, bf16[384,384]{1,0:T(8,128)(2,1)S(1)} %get-tuple-element.19.refs_1_, ...), custom_call_target="tpu_custom_call" | custom-call | tf_op jit(solution)/shard_map/results/pallas_call | solution.py:792

commit v4 on v3

--- a/solution.py
+++ b/solution.py
@@ -459,8 +459,9 @@
         slot = tg.at[x, yh]
         return remote(slot, slot, r_["tgs"].at[0], r_["tgr"].at[0], {"sp": me_sp ^ 4})
 
-    def tz_copy(j):
-        return remote(tg.at[x], tg.at[x], r_["tzs"].at[0], r_["tzr"].at[0], along_x(j))
+    def tz_copy(i, j):
+        slot = tg.at[x, i]
+        return remote(slot, slot, r_["tzs"].at[0], r_["tzr"].at[0], along_x(j))
 
     def text_1():
         all_of(tx_in, r_["txs"].at[0], r_["txr"].at[0]).wait_recv()
@@ -479,11 +480,13 @@
         ty_copy().wait_recv()
         tg[x, yh] = (t_own[...] + ty_in[...].astype(f32)).astype(bf16)
         tg_copy().start()
+        for j in range(1, 4):
+            tz_copy(yh, j).start()
 
     def text_3():
         tg_copy().wait_recv()
         for j in range(1, 4):
-            tz_copy(j).start()
+            tz_copy(1 - yh, j).start()
 
     def text_4():
         all_of(tx_in, r_["tzs"].at[0], r_["tzr"].at[0]).wait_recv()
@@ -588,34 +591,6 @@
     gw_s1(4)
     for r in (0, 1, 7):
         gw_sy(r)
-    for j in range(1, 4):
-        tx_copy(j).start()
-    for r in (2, 6):
-        gw_sy(r)
-    halo_start([4 * heads + 1, 3 * heads])
-    own_part(0)
-    for r in (0, 1, 7):
-        gw_sx(r)
-    for r in (3, 5):
-        gw_sy(r)
-    halo_start([3 * heads + 1])
-    own_part(1)
-    gw_sy(4)
-    halo_start([3 * heads + 2])
-    own_part(2)
-    text_1()
-    halo_wait_both(("st", 0), ("q", 0))
-    for h in range(heads):
-        for side in (0, 1):
-            pl.when(has[side])(functools.partial(far_weights, side, h))
-    for r in (2, 6):
-        gw_sx(r)
-    for r in (0, 1, 7):
-        gw_ag(r)
-    text_2()
-    for r in (3, 5):
-        gw_sx(r)
-
     def far_head(h):
         halo_wait_both(("ga", h))
         for side in (0, 1):
@@ -624,16 +599,43 @@
         gk_v[:, c] = (factor * gk_sum[:, c]).astype(bf16)
         gv_v[:, c] = gv_sum[:, c].astype(bf16)
 
+    for j in range(1, 4):
+        tx_copy(j).start()
+    for r in (2, 6):
+        gw_sy(r)
+    own_part(0)
+    for r in (0, 1, 7):
+        gw_sx(r)
+    for r in (3, 5):
+        gw_sy(r)
+    halo_start([4 * heads + 1, 3 * heads])
+    own_part(1)
+    gw_sy(4)
+    own_part(2)
+    halo_start([3 * heads + 1])
+    for r in (2, 6):
+        gw_sx(r)
+    text_1()
+    halo_wait_both(("st", 0), ("q", 0))
+    for h in range(heads):
+        for side in (0, 1):
+            pl.when(has[side])(functools.partial(far_weights, side, h))
+    for r in (3, 5):
+        gw_sx(r)
+    gw_sx(4)
+    halo_start([3 * heads + 2])
+    text_2()
+    for r in (0, 1, 7):
+        gw_ag(r)
+    for r in (2, 6):
+        gw_ag(r)
     halo_wait_both(("dl", 0))
     far_head(0)
-    gw_sx(4)
-    for r in (2, 6):
-        gw_ag(r)
-    far_head(1)
     for r in (3, 5):
         gw_ag(r)
+    gw_ag(4)
     text_3()
-    gw_ag(4)
+    far_head(1)
     far_head(2)
     text_4()
     for r in (0, 1, 7, 2, 6, 3, 5, 4):

time: 67.1 us -> 65.7 us (0.979)
  Pallas kernels: 64.5 us -> 63.2 us
    pallas_call x1, Pallas kernels: 63 us -> 61.7 us  [call(): pl.pallas_call(functools.partial(kernel, tuple(names)), out_shape=[pltpu....]
where the time goes in v4:
time: 65.7 us; the launch traced here: 64.6 us
  Pallas kernels  63.2 us (96%)
  between operations  1.45 us (2%)
    pallas_call x1, Pallas kernels, call(): pl.pallas_call(functools.partial(kernel, tuple(names)), out_shape=[pltpu....  61.7 us
    pallas_call x1, Pallas kernels, copy_call(): pl.pallas_call(functools.partial(copy_kernel, n), out_shape=[jax.ShapeDty...  1.49 us

profile of v4, /device:TPU:8, one launch (start us, length us, event | category | flops | bytes accessed | tf_op | source)
XLA Modules:
  0.0 64.6 jit_solution(17210094448904021631)
XLA Ops:
  1.3 61.7 %attention_backward.1 = (bf16[384,384]{1,0:T(8,128)(2,1)S(1)}, bf16[384,384]{1,0:T(8,128)(2,1)S(1)}, bf16[384,384]{1,0:T(8,128)(2,1)S(1)}, bf16[256,384]{1,0:T(8...) custom-call(bf16[384,384]{1,0:T(8,128)(2,1)} %bitcast.12, bf16[384,384]{1,0:T(8,128)(2,1)} %bitcast.13, ...), custom_call_target="tpu_custom_call" | custom-call | tf_op jit(solution)/shard_map/attention_backward/pallas_call | solution.py:769
  63.0 1.5 %results.1 = (bf16[384,384]{1,0:T(8,128)(2,1)}, bf16[384,384]{1,0:T(8,128)(2,1)}, bf16[384,384]{1,0:T(8,128)(2,1)}, bf16[256,384]{1,0:T(8,128)(2,1)}, bf16[256,384]{1,0:T(8,128)(2,1)}, /*index=5*/f32[384,768]{1,0:T(8,128)}) custom-call(bf16[384,384]{1,0:T(8,128)(2,1)S(1)} %get-tuple-element.18.refs_0_, bf16[384,384]{1,0:T(8,128)(2,1)S(1)} %get-tuple-element.19.refs_1_, ...), custom_call_target="tpu_custom_call" | custom-call | tf_op jit(solution)/shard_map/results/pallas_call | solution.py:794

commit v5 on v4

--- a/solution.py
+++ b/solution.py
@@ -277,7 +277,7 @@
         side_bias.append(jnp.minimum(jnp.where(seen, 0.0, -1e30).astype(f32), edge))
     place_of = lax.broadcasted_iota(jnp.int32, (text, 1), 0)
     words = jnp.where(place_of < live_ref[0], 0.0, -1e30).astype(f32)
-    bias_ref = r_["bias"]
+    bias_ref, st_near = r_["bias"], r_["st_near"]
     bias_ref[:tok] = jnp.zeros((tok, 1), f32)
     bias_ref[tok:near] = words
     for side in (0, 1):
@@ -287,15 +287,30 @@
     def cols(h):
         return slice(h * HD, (h + 1) * HD)
 
+    def near_scores(h):
+        c = cols(h)
+        scores = factor * mm(keys[:near, c], q_ref[:, c], NT) + bias_ref[:near]
+        top = jnp.max(scores, axis=0, keepdims=True)
+        e = jnp.exp(scores - top)
+        wts[h, :near, :] = e
+        st_near[h : h + 1, :] = top
+        st_near[heads + h : heads + h + 1, :] = jnp.sum(e, axis=0, keepdims=True)
+
     def forward(h):
         c = cols(h)
-        scores = factor * mm(keys[:, c], q_ref[:, c], NT) + bias_ref[...]
-        top = jnp.max(scores, axis=0, keepdims=True)
+        scores = factor * mm(keys[near:, c], q_ref[:, c], NT) + bias_ref[near:]
+        top_near = st_near[h : h + 1, :]
+        top = jnp.maximum(top_near, jnp.max(scores, axis=0, keepdims=True))
         e = jnp.exp(scores - top)
-        inv = 1.0 / jnp.sum(e, axis=0, keepdims=True)
-        weights = e * inv
-        wts[h] = weights
-        att_t[c, :] = mm(vals[:, c], weights.astype(bf16), TN).astype(bf16)
+        fix = jnp.exp(top_near - top)
+        total = jnp.sum(e, axis=0, keepdims=True) + fix * st_near[heads + h : heads + h + 1, :]
+        inv = 1.0 / total
+        w_near = wts[h, :near, :] * (fix * inv)
+        w_far = e * inv
+        wts[h, :near, :] = w_near
+        wts[h, near:, :] = w_far
+        att = mm(vals[:near, c], w_near.astype(bf16), TN) + mm(vals[near:, c], w_far.astype(bf16), TN)
+        att_t[c, :] = att.astype(bf16)
         for side in (0, 1):
             st_out[side, h : h + 1, :] = top - side_bias[side]
             st_out[side, heads + h : heads + h + 1, :] = inv
@@ -533,6 +548,8 @@
         gv_sum[:, c] += mm(weights.astype(bf16), ga, NT)
 
     scale(0)
+    for h in range(heads):
+        near_scores(h)
     z_arrive(0, 0)
     z_arrive(0, 1)
     scale(1)
@@ -554,29 +571,30 @@
     for r in (0, 1, 7):
         gw_part(r)
     z_arrive(2, 0)
-    gw_s1(0)
-    gw_s1(1)
+    for r in (2, 6):
+        gw_part(r)
+    for r in (0, 1, 7):
+        gw_s1(r)
     w_fwd().wait_recv()
     ga_add(0, True)
-    gw_s1(7)
+    ga_add(1)
     for r in (2, 6):
-        gw_part(r)
-    ga_add(1)
+        gw_s1(r)
     ga_add(7)
     ga_add(2)
     z_arrive(2, 1)
-    ga_add(6)
     scale(3)
     scale(5)
+    for r in (3, 5):
+        gw_part(r)
+    ga_add(6)
     ga_add(3)
     ga_add(5)
-    for r in (3, 5):
-        gw_part(r)
-    for r in (2, 6):
-        gw_s1(r)
     z_arrive(3, 0)
     scale(4)
     gw_part(4)
+    for r in (3, 5):
+        gw_s1(r)
     ga_add(4)
     ga_t[...] = acc[...].astype(bf16)
     for h in range(heads):
@@ -584,11 +602,9 @@
         dl_out[h : h + 1, :] = jnp.sum(
             ga_t[c, :].astype(f32) * att_t[c, :].astype(f32), axis=0, keepdims=True
         )
-    for r in (3, 5):
-        gw_s1(r)
+    gw_s1(4)
     for h in range(heads):
         text_part(h)
-    gw_s1(4)
     for r in (0, 1, 7):
         gw_sy(r)
     def far_head(h):
@@ -604,12 +620,12 @@
     for r in (2, 6):
         gw_sy(r)
     own_part(0)
+    own_part(1)
+    for r in (3, 5):
+        gw_sy(r)
     for r in (0, 1, 7):
         gw_sx(r)
-    for r in (3, 5):
-        gw_sy(r)
     halo_start([4 * heads + 1, 3 * heads])
-    own_part(1)
     gw_sy(4)
     own_part(2)
     halo_start([3 * heads + 1])
@@ -709,6 +725,7 @@
         ("dl_out", (8, tok), f32),
         ("dl_in", (2, 8, tok), f32),
         ("bias", (total, 1), f32),
+        ("st_near", (8, tok), f32),
         ("raw", (8, tok, block), bf16),
         ("nat", (8, tok, block), bf16),
         ("w_all", (4, width, cols), bf16),

time: 65.7 us -> 65.1 us (level)
  Pallas kernels: 63.2 us -> 62.4 us
    pallas_call x1, Pallas kernels: 61.7 us -> 60.9 us  [call(): pl.pallas_call(functools.partial(kernel, tuple(names)), out_shape=[pltpu....]
where the time goes in v5:
time: 65.1 us; the launch traced here: 63.9 us
  Pallas kernels  62.4 us (96%)
  between operations  1.45 us (2%)
    pallas_call x1, Pallas kernels, call(): pl.pallas_call(functools.partial(kernel, tuple(names)), out_shape=[pltpu....  60.9 us
    pallas_call x1, Pallas kernels, copy_call(): pl.pallas_call(functools.partial(copy_kernel, n), out_shape=[jax.ShapeDty...  1.49 us

profile of v5, /device:TPU:8, one launch (start us, length us, event | category | flops | bytes accessed | tf_op | source)
XLA Modules:
  0.0 63.9 jit_solution(4249701791717838304)
XLA Ops:
  1.3 60.9 %attention_backward.1 = (bf16[384,384]{1,0:T(8,128)(2,1)S(1)}, bf16[384,384]{1,0:T(8,128)(2,1)S(1)}, bf16[384,384]{1,0:T(8,128)(2,1)S(1)}, bf16[256,384]{1,0:T(8...) custom-call(bf16[384,384]{1,0:T(8,128)(2,1)} %bitcast.12, bf16[384,384]{1,0:T(8,128)(2,1)} %bitcast.13, ...), custom_call_target="tpu_custom_call" | custom-call | tf_op jit(solution)/shard_map/attention_backward/pallas_call | solution.py:786
  62.2 1.5 %results.1 = (bf16[384,384]{1,0:T(8,128)(2,1)}, bf16[384,384]{1,0:T(8,128)(2,1)}, bf16[384,384]{1,0:T(8,128)(2,1)}, bf16[256,384]{1,0:T(8,128)(2,1)}, bf16[256,384]{1,0:T(8,128)(2,1)}, /*index=5*/f32[384,768]{1,0:T(8,128)}) custom-call(bf16[384,384]{1,0:T(8,128)(2,1)S(1)} %get-tuple-element.18.refs_0_, bf16[384,384]{1,0:T(8,128)(2,1)S(1)} %get-tuple-element.19.refs_1_, ...), custom_call_target="tpu_custom_call" | custom-call | tf_op jit(solution)/shard_map/results/pallas_call | solution.py:811

commit v6 on v5

--- a/solution.py
+++ b/solution.py
@@ -321,6 +321,9 @@
         e = jnp.exp(scores - st_in[side, h : h + 1, :])
         wfar[side, h] = e * st_in[side, heads + h : heads + h + 1, :]
 
+    def own_slot(r):
+        return 2 * (blk(r) >> 2) + (blk(r) & 1)
+
     def core_owns(r):
         return ((blk(r) >> 1) & 1) == core
 
@@ -329,7 +332,7 @@
 
     def s1_copy(r):
         return remote(
-            g1_out.at[r], g1_in.at[r], r_["s1s"].at[0], r_["s1r"].at[r], {"dp": me_dp ^ 1}
+            g1_out.at[r], g1_in.at[r], r_["s1s"].at[0], r_["s1r"].at[own_slot(r)], {"dp": me_dp ^ 1}
         )
 
     def x_first(r):
@@ -353,7 +356,7 @@
             gy_out.at[r, place1(r) ^ j],
             gy_in.at[r, j - 1],
             r_["gys"].at[0],
-            r_["gyr"].at[r],
+            r_["gyr"].at[own_slot(r)],
             where,
         )
 
@@ -363,20 +366,20 @@
             gx_out.at[r, place2(r) ^ j],
             gx_in.at[r, j - 1],
             r_["gxs"].at[0],
-            r_["gxr"].at[r],
+            r_["gxr"].at[own_slot(r)],
             where,
         )
 
     def ag1_copy(r, j):
         piece_ = gall.at[r, x]
-        return remote(piece_, piece_, r_["ag1s"].at[0], r_["ag1r"].at[r], along_x(j))
+        return remote(piece_, piece_, r_["ag1s"].at[0], r_["ag1r"].at[own_slot(r)], along_x(j))
 
     def ag2_copy(r, i):
         return remote(
             gall.at[r],
             gfin.at[blk(r) & 1, y],
             r_["ag2s"].at[0],
-            r_["ag2r"].at[r],
+            r_["ag2r"].at[blk(r) & 1],
             {"dp": blk(r) >> 1, "sp": 4 * i + x},
         )
 
@@ -410,7 +413,7 @@
     def gw_sy(r):
         @pl.when(core_owns(r))
         def _():
-            all_of(gy_in.at[r], r_["gys"].at[0], r_["gyr"].at[r]).wait_recv()
+            all_of(gy_in.at[r], r_["gys"].at[0], r_["gyr"].at[own_slot(r)]).wait_recv()
             for k in range(4):
                 at = pl.multiple_of(place1(r) * (4 * piece) + k * piece, 8)
                 total = parts[r, pl.ds(at, piece), :]
@@ -424,7 +427,7 @@
     def gw_sx(r):
         @pl.when(core_owns(r))
         def _():
-            all_of(gx_in.at[r], r_["gxs"].at[0], r_["gxr"].at[r]).wait_recv()
+            all_of(gx_in.at[r], r_["gxs"].at[0], r_["gxr"].at[own_slot(r)]).wait_recv()
             total = parts[r, pl.ds(pl.multiple_of(place2(r) * piece, 8), piece), :]
             for j in range(3):
                 total = total + gx_in[r, j].astype(f32)
@@ -435,7 +438,7 @@
     def gw_ag(r):
         @pl.when(core_owns(r))
         def _():
-            all_of(gx_in.at[0], r_["ag1s"].at[0], r_["ag1r"].at[r]).wait_recv()
+            all_of(gx_in.at[0], r_["ag1s"].at[0], r_["ag1r"].at[own_slot(r)]).wait_recv()
 
         for i in (0, 1):
 
@@ -452,7 +455,7 @@
     def gw_end(r):
         @pl.when(mine(r))
         def _():
-            all_of(gy_in.at[0], r_["ag2s"].at[0], r_["ag2r"].at[r]).wait_recv()
+            all_of(gy_in.at[0], r_["ag2s"].at[0], r_["ag2r"].at[blk(r) & 1]).wait_recv()
             at = pl.ds(pl.multiple_of((blk(r) & 1) * w, HD), w)
             for i in range(4):
                 for k in range(4):
@@ -761,15 +764,15 @@
         ("hs", (2, 3)),
         ("hr", (2, 2 * heads + 3)),
         ("s1s", (1,)),
-        ("s1r", (8,)),
+        ("s1r", (4,)),
         ("gys", (1,)),
-        ("gyr", (8,)),
+        ("gyr", (4,)),
         ("gxs", (1,)),
-        ("gxr", (8,)),
+        ("gxr", (4,)),
         ("ag1s", (1,)),
-        ("ag1r", (8,)),
+        ("ag1r", (4,)),
         ("ag2s", (1,)),
-        ("ag2r", (8,)),
+        ("ag2r", (2,)),
         ("txs", (1,)),
         ("txr", (1,)),
         ("tys", (1,)),

time: 65.1 us -> 64.9 us (level)
  no operation moved by 1% of the time
where the time goes in v6:
time: 64.9 us; the launch traced here: 63.7 us
  Pallas kernels  62.3 us (96%)
  between operations  1.45 us (2%)
    pallas_call x1, Pallas kernels, call(): pl.pallas_call(functools.partial(kernel, tuple(names)), out_shape=[pltpu....  60.8 us
    pallas_call x1, Pallas kernels, copy_call(): pl.pallas_call(functools.partial(copy_kernel, n), out_shape=[jax.ShapeDty...  1.49 us

profile of v6, /device:TPU:8, one launch (start us, length us, event | category | flops | bytes accessed | tf_op | source)
XLA Modules:
  0.0 63.7 jit_solution(17214318902982329097)
XLA Ops:
  1.3 60.8 %attention_backward.1 = (bf16[384,384]{1,0:T(8,128)(2,1)S(1)}, bf16[384,384]{1,0:T(8,128)(2,1)S(1)}, bf16[384,384]{1,0:T(8,128)(2,1)S(1)}, bf16[256,384]{1,0:T(8...) custom-call(bf16[384,384]{1,0:T(8,128)(2,1)} %bitcast.12, bf16[384,384]{1,0:T(8,128)(2,1)} %bitcast.13, ...), custom_call_target="tpu_custom_call" | custom-call | tf_op jit(solution)/shard_map/attention_backward/pallas_call | solution.py:789
  62.1 1.5 %results.1 = (bf16[384,384]{1,0:T(8,128)(2,1)}, bf16[384,384]{1,0:T(8,128)(2,1)}, bf16[384,384]{1,0:T(8,128)(2,1)}, bf16[256,384]{1,0:T(8,128)(2,1)}, bf16[256,384]{1,0:T(8,128)(2,1)}, /*index=5*/f32[384,768]{1,0:T(8,128)}) custom-call(bf16[384,384]{1,0:T(8,128)(2,1)S(1)} %get-tuple-element.18.refs_0_, bf16[384,384]{1,0:T(8,128)(2,1)S(1)} %get-tuple-element.19.refs_1_, ...), custom_call_target="tpu_custom_call" | custom-call | tf_op jit(solution)/shard_map/results/pallas_call | solution.py:814
